TPU v7x, 32 devices: a whole 2x2x4 slice. The times are simulated.
32 devices in a mesh: dp: 4 (over y, core), mp: 8 (over z, x).
Axes of the slice: x: 2, y: 2, z: 4, core: 2. Of those that a mesh axis runs over, the one named last changes fastest.
Arguments:
- tokens: bfloat16 [9216, 1024], P(('dp', 'mp')), may hold values from -6 to 6
- image_ids: int32 [9216], P('dp'), may hold values from 0 to 1, as said below
- lengths: int32 [4, 2], P('dp'), may hold values from 0 to 2304, as said below
- w_qkv: bfloat16 [3, 1024, 1024], P(None, None, 'mp'), may hold values from -0.1875 to 0.1875
- bias_query: float32 [1024], P('mp'), may hold values from -3 to 3
- bias_value: float32 [1024], P('mp'), may hold values from -0.3 to 0.3
- w_out: bfloat16 [1024, 1024], P('mp'), may hold values from -3 to 3
- w_up: bfloat16 [1024, 4096], P(None, 'mp'), may hold values from -0.1875 to 0.1875
- bias_up: float32 [4096], P('mp'), may hold values from -3 to 3
- w_down: bfloat16 [4096, 1024], P('mp'), may hold values from -0.09375 to 0.09375
- out_biases: float32 [2, 1024], replicated, may hold values from -2 to 2
- norm_gain: float32 [2, 1024], replicated, may hold values from 0.25 to 1.75
- norm_bias: float32 [2, 1024], replicated, may hold values from -2 to 2
- cotangent: bfloat16 [9216, 1024], P(('dp', 'mp')), may hold values from -6 to 6
Outputs:
- output: bfloat16 [9216, 1024], P(('dp', 'mp'))
- input_grad: bfloat16 [9216, 1024], P(('dp', 'mp'))
- grad_w_qkv: float32 [3, 1024, 1024], P(None, None, 'mp')
- grad_bias_query: float32 [1024], P('mp')
- grad_bias_value: float32 [1024], P('mp')
- grad_w_out: float32 [1024, 1024], P('mp')
- grad_w_up: float32 [1024, 4096], P(None, 'mp')
- grad_bias_up: float32 [4096], P('mp')
- grad_w_down: float32 [4096, 1024], P('mp')
- grad_out_biases: float32 [2, 1024], replicated
- grad_norm_gain: float32 [2, 1024], replicated
- grad_norm_bias: float32 [2, 1024], replicated
Inputs may be any that keep to these rules, and one draw needn't show every extreme that they name: `image_ids`: within each group of 2304 rows (one group for each index of dp) the image numbers never fall: a group holds either one image over all its rows, or two images of 1152 rows each. lengths[g, k] counts the valid rows at the start of image k of group g: 2304 for an image that fills its group (the second entry is then 0), else 1024. Some group holds an image of 2304 rows.
All inputs are finite; a program needn't handle non-finite values.
Results may differ from a plain program's by a relative error of at most 0.02.
Values may be sent and summed in bfloat16 or wider, within the bound.
A program may use at most 128 MiB of HBM per device.

v0:
```python
import functools
import types

import jax
import jax.numpy as jnp
from jax import lax
from jax.experimental import pallas as pl
from jax.experimental.pallas import tpu as pltpu
from jax.sharding import PartitionSpec as P

HEAD_DIM = 64
LANES = 128
CHUNK = 768
MASKED = -1e30
MESH = pl.DeviceIdType.MESH
VMEM_BYTES = 67_043_328
BF = jnp.bfloat16
F32 = jnp.float32
NN = (((1,), (0,)), ((), ()))
NT = (((1,), (1,)), ((), ()))
TN = (((0,), (0,)), ((), ()))
SCALE = HEAD_DIM ** (-0.5)
PARTS = 4
epsilon = 1e-06


def dot(left, right, dims=NN):
    return lax.dot_general(left, right, dims, preferred_element_type=F32)


def layer_norm(values, gain_vec, shift_vec):
    row_mean = jnp.mean(values, axis=-1, keepdims=True)
    centered = values - row_mean
    variance = jnp.mean(centered * centered, axis=-1, keepdims=True)
    return centered * lax.rsqrt(variance + epsilon) * gain_vec + shift_vec


def exact_gelu(values):
    return jax.nn.gelu(values, approximate=False)


def mp_parts(n):
    chain = min(4, n)
    return chain, n // chain


def column_sum(values):
    ones = jnp.ones((8, values.shape[1]), BF)
    high = values.astype(BF)
    low = (values - high.astype(F32)).astype(BF)
    return dot(ones, high, NT) + dot(ones, low, NT)


def split_three(column):
    high = column.astype(BF)
    rest = column - high.astype(F32)
    middle = rest.astype(BF)
    return high, middle, (rest - middle.astype(F32)).astype(BF)


def attend_chunk(c, heads, q_ref, k_ref, v_ref, vt_ref, self_ref, att_ref, lse_ref):
    rows = pl.ds(pl.multiple_of(c * CHUNK, CHUNK), CHUNK)
    pieces = []
    scores = [dot(k_ref[h], q_ref[h, rows, :], NT) for h in range(heads)]
    for h in range(heads):
        own = q_ref[h, rows, :HEAD_DIM].astype(F32) * k_ref[h, rows, :HEAD_DIM].astype(F32)
        own = column_sum(own)[:1] + self_ref[:1, rows]
        top = jnp.maximum(jnp.max(scores[h], axis=0, keepdims=True), own)
        weights = jnp.exp(scores[h] - top).astype(BF)
        own_weight = jnp.exp(own - top).astype(BF).astype(F32)
        summed = dot(vt_ref[h], weights) + vt_ref[h, :, rows].astype(F32) * own_weight
        total = summed[HEAD_DIM : HEAD_DIM + 1]
        pieces.append(summed[:HEAD_DIM] / total)
        lse_ref[h, :, rows] = jnp.broadcast_to(top + jnp.log(total), (8, CHUNK))
    stacked = jnp.concatenate(pieces, axis=0) if heads > 1 else pieces[0]
    att_ref[rows, :] = stacked.T.astype(BF)


def front_kernel(
    n,
    ids_ref,
    lengths_ref,
    tokens_ref,
    cot_ref,
    gain_ref,
    shift_ref,
    out_bias_ref,
    w_ref,
    bias_ref,
    up_ref,
    down_ref,
    out_ref,
    bup_ref,
    normed_ref,
    q_ref,
    k_ref,
    v_ref,
    lse_ref,
    att_ref,
    owned_ref,
    ups_ref,
    downs_ref,
    outs_out,
    bups_ref,
    peers_ref,
    self_ref,
    hidden_ref,
    pair_two,
    pair_cot,
    blocks,
    outs_ref,
    two,
    cot,
    peer_w,
    peer_b,
    proj_out,
    proj_in,
    vt_ref,
    owned,
    ssz,
    rsz,
    ssx,
    rsx,
    spw,
    rpw,
    spb,
    rpb,
    ssa,
    rsa,
    wsz,
    wrz,
    wsx,
    wrx,
    gs,
    gr,
    os,
    orr,
    bs,
    br,
    spp,
    rpp,
    local_sem,
):
    chain, cols = mp_parts(n)
    share, _ = tokens_ref.shape
    width = w_ref.shape[2]
    heads = width // HEAD_DIM
    hidden = up_ref.shape[1]
    up_rows, down_rows, out_rows = (r.shape[0] // PARTS for r in (up_ref, down_ref, out_ref))
    dg, dp = lax.axis_index("dg"), lax.axis_index("dp")
    a, b = lax.axis_index("mz"), lax.axis_index("mx")
    me = a * cols + b
    part = lax.rem(dp, PARTS)
    core_dp = dp + 1 - 2 * lax.rem(dp, 2)
    side_dp = dp + 2 - 4 * lax.rem(dp // 2, 2)
    core_part, side_part = lax.rem(core_dp, PARTS), lax.rem(side_dp, PARTS)
    far_part = PARTS - 1 - part

    barrier = pltpu.get_barrier_semaphore()
    for off in range(1, n):
        other = lax.rem(me + off, n)
        pl.semaphore_signal(
            barrier,
            inc=1,
            device_id=(dg, dp, other // cols, lax.rem(other, cols)),
            device_id_type=MESH,
        )
    for peer in (core_dp, side_dp):
        pl.semaphore_signal(barrier, inc=1, device_id=(dg, peer, a, b), device_id_type=MESH)
    pl.semaphore_wait(barrier, n + 1)

    def remote(src, dst, send, recv, device):
        return pltpu.make_async_remote_copy(
            src_ref=src,
            dst_ref=dst,
            send_sem=send,
            recv_sem=recv,
            device_id=(dg,) + device,
            device_id_type=MESH,
        )

    def span(index, size):
        return pl.ds(pl.multiple_of(index * size, size), size)

    def can(way):
        return (a < chain - 1) if way == 0 else (a > 0)

    def chain_peer(way):
        return (dp, jnp.clip(a + (1 if way == 0 else -1), 0, chain - 1), b)

    def cross_peer(off):
        return (dp, a, lax.rem(b + off, cols))

    def back_peer(off):
        return (dp, a, lax.rem(b - off + cols, cols))

    def chain_copy(row, way):
        spot = blocks.at[row]
        return remote(spot, spot, ssz.at[way, row], rsz.at[way, row], chain_peer(way))

    def cross_copy(row, off):
        return remote(
            proj_out.at[off - 1, row],
            proj_in.at[off - 1, row],
            ssx.at[off, row],
            rsx.at[off, row],
            back_peer(off),
        )

    def peer_copies(off):
        return [
            remote(w_ref, peer_w.at[off - 1], spw.at[off], rpw.at[off], cross_peer(off)),
            remote(bias_ref, peer_b.at[off - 1], spb.at[off], rpb.at[off], cross_peer(off)),
        ]

    def piece(i, row, of_part):
        if i == 0:
            return outs_ref.at[row * cols + b, span(of_part, out_rows)]
        if i == 1:
            return ups_ref.at[span(of_part, up_rows), span(row, hidden)]
        return downs_ref.at[span(row * PARTS + of_part, down_rows)]

    def own_piece(i):
        if i == 0:
            return out_ref.at[span(part, out_rows)]
        if i == 1:
            return up_ref.at[span(part, up_rows)]
        return down_ref.at[span(part, down_rows)]

    def weight_copy(i, row, way, own=False):
        spot = piece(i, row, part)
        sems = wsz.at[i, way, row], wrz.at[i, way, row]
        return remote(own_piece(i) if own else spot, spot, *sems, chain_peer(way))

    def out_cross(block, off, own=False):
        spot = outs_ref.at[block, span(part, out_rows)]
        sems = wsx.at[off, block // cols], wrx.at[off, block // cols]
        return remote(own_piece(0) if own else spot, spot, *sems, cross_peer(off))

    def group_copy(kind, i, row, arriving=False):
        sent = side_part if kind == 2 else part
        got = (side_part, core_part, far_part)[kind]
        spot = piece(i, row, got if arriving else sent)
        sems = gs.at[kind, i - 1, row], gr.at[kind, i - 1, row]
        return remote(spot, spot, *sems, (side_dp if kind == 0 else core_dp, a, b))

    def out_group(kind, arriving=False):
        sent = side_part if kind == 2 else part
        got = (side_part, core_part, far_part)[kind]
        spot = outs_ref.at[:, span(got if arriving else sent, out_rows)]
        return remote(spot, spot, os.at[kind], orr.at[kind], (side_dp if kind == 0 else core_dp, a, b))

    def bias_copy(off, arriving=False):
        spot = bups_ref.at[lax.rem(a - off + chain, chain) if arriving else a]
        return remote(bup_ref, spot, bs.at[off], br.at[off], (dp, lax.rem(a + off, chain), b))

    def start_own(way):
        for i in (1, 2):
            weight_copy(i, a, way, own=True).start()

    stay = [
        pltpu.make_async_copy(up_ref, ups_ref.at[:, span(a, hidden)], local_sem.at[1]),
        pltpu.make_async_copy(down_ref, downs_ref.at[span(a, hidden)], local_sem.at[2]),
        pltpu.make_async_copy(own_piece(0), piece(0, a, part), local_sem.at[3]),
        pltpu.make_async_copy(bup_ref, bups_ref.at[a], local_sem.at[4]),
    ]

    for off in range(1, cols):
        for copy in peer_copies(off):
            copy.start()
    normed = layer_norm(tokens_ref[...].astype(F32), gain_ref[:1], shift_ref[:1])
    blocks[a] = normed.astype(BF)

    total = n * share
    slot = total // 2
    first_id, last_id = ids_ref[0], ids_ref[total - 1]
    first_length, last_length = (
        jnp.where(k == 0, lengths_ref[0, 0], lengths_ref[0, 1]) for k in (first_id, last_id)
    )
    last_start = jnp.where(first_id == last_id, 0, slot)

    def row_facts(index):
        late = index >= slot
        inside = index - jnp.where(late, last_start, 0) < jnp.where(late, last_length, first_length)
        return jnp.where(late, last_id, first_id), inside

    def place(block, out_q, out_k, out_v):
        rows = span(block, share)
        lane = lax.broadcasted_iota(jnp.int32, (share, LANES - HEAD_DIM), 1)
        image, inside = row_facts(
            block * share + lax.broadcasted_iota(jnp.int32, (share, LANES - HEAD_DIM), 0)
        )
        tail_q = jnp.where(lane == image, 1.0, 0.0).astype(BF)
        hidden_key = jnp.where((lane == image) & inside, 0.0, MASKED)
        tail_k = jnp.where(lane < 2, hidden_key, 0.0).astype(BF)
        tail_v = jnp.where(lane < 3, 1.0, 0.0).astype(BF)
        for h in range(heads):
            cut = slice(h * HEAD_DIM, (h + 1) * HEAD_DIM)
            q_ref[h, rows, :] = jnp.concatenate(
                [out_q[:, cut] * jnp.asarray(SCALE, BF), tail_q], axis=1
            )
            k_ref[h, rows, :] = jnp.concatenate([out_k[:, cut], tail_k], axis=1)
            v_ref[h, rows, :] = jnp.concatenate([out_v[:, cut], tail_v], axis=1)

    def project(row):
        values = blocks[row]
        place(
            row * cols + b,
            (dot(values, w_ref[0]) + bias_ref[0, :1]).astype(BF),
            dot(values, w_ref[1]).astype(BF),
            (dot(values, w_ref[2]) + bias_ref[1, :1]).astype(BF),
        )

    def project_peer(row):
        def one(slot, _):
            values = blocks[row]
            proj_out[slot, row, 0] = (dot(values, peer_w[slot, 0]) + peer_b[slot, 0, :1]).astype(BF)
            proj_out[slot, row, 1] = dot(values, peer_w[slot, 1]).astype(BF)
            proj_out[slot, row, 2] = (dot(values, peer_w[slot, 2]) + peer_b[slot, 1, :1]).astype(BF)
            return 0

        lax.fori_loop(0, cols - 1, one, 0)
        for off in range(1, cols):
            cross_copy(row, off).start()

    for way in (0, 1):

        @pl.when(can(way))
        def _(way=way):
            chain_copy(a, way).start()
            weight_copy(0, a, way, own=True).start()

    def pair_copy(i, off):
        src, dst = ((two, pair_two), (cot, pair_cot))[i]
        return remote(src, dst.at[off], spp.at[i, off], rpp.at[i, off], cross_peer(off))

    pair_stay = [
        pltpu.make_async_copy(two, pair_two.at[0], local_sem.at[6]),
        pltpu.make_async_copy(cot, pair_cot.at[0], local_sem.at[7]),
    ]
    for copy in stay:
        copy.start()

    @pl.when(a == 0)
    def _():
        start_own(0)

    @pl.when(a == chain - 1)
    def _():
        start_own(1)

    project(a)
    _, self_inside = row_facts(lax.broadcasted_iota(jnp.int32, (8, total), 1))
    self_ref[...] = jnp.where(self_inside, MASKED, 0.0)

    def mask_cot(i, _):
        cut = span(i, 16)
        _, inside = row_facts(
            me * share + i * 16 + lax.broadcasted_iota(jnp.int32, (16, cot.shape[1]), 0)
        )
        cot[cut, :] = jnp.where(inside, cot_ref[cut, :].astype(F32), 0.0).astype(BF)
        return 0

    lax.fori_loop(0, share // 16, mask_cot, 0)

    def visit(step, _):
        for way in (0, 1):
            there = a - step if way == 0 else a + step
            inside = (there >= 0) & (there < chain)
            row = jnp.clip(there, 0, chain - 1)

            @pl.when(inside)
            def _(way=way, row=row):
                chain_copy(row, way).wait_recv()

                @pl.when(can(way))
                def _():
                    chain_copy(row, way).start()

                weight_copy(0, row, way).wait_recv()

                @pl.when(can(way))
                def _():
                    weight_copy(0, row, way).start()

        @pl.when((step == a) & can(0))
        def _():
            start_own(0)

        @pl.when((step == chain - 1 - a) & can(1))
        def _():
            start_own(1)

        @pl.when(step == 1)
        def _():
            for off in range(1, cols):
                for copy in peer_copies(off):
                    copy.wait_recv()

        def one(j, _):
            gone = step - jnp.where(j == 0, 1, 0)
            there = jnp.where(j == 1, a - gone, a + gone)

            @pl.when((there >= 0) & (there < chain) & ((j > 0) | (step == 1)))
            def _():
                @pl.when(j > 0)
                def _():
                    project(there)

                project_peer(there)

            return 0

        lax.fori_loop(0, 3, one, 0)
        return 0

    lax.fori_loop(1, chain, visit, 0)

    stay[2].wait()
    for off in range(1, cols):
        out_cross(me, off, own=True).start()

    def out_send(i, _):
        row = lax.rem(a + i, chain)
        for off in range(1, cols):
            out_cross(row * cols + b, off).start()
        return 0

    lax.fori_loop(1, chain, out_send, 0)

    def receive(i, _):
        row = lax.rem(a + i, chain)
        for off in range(1, cols):
            cross_copy(row, off).wait_recv()
            block = row * cols + lax.rem(b + off, cols)
            place(block, *[proj_in[off - 1, row, t] for t in range(3)])
        return 0

    lax.fori_loop(0, chain, receive, 0)
    keep = pltpu.make_async_copy(blocks, normed_ref, local_sem.at[0])
    keep.start()
    keep_peers = pltpu.make_async_copy(peer_w, peers_ref, local_sem.at[5])
    keep_peers.start()

    def gather_out(row, _):
        for off in range(1, cols):
            out_cross(row * cols + lax.rem(b - off + cols, cols), off).wait_recv()
        return 0

    lax.fori_loop(0, chain, gather_out, 0)
    out_group(0).start()
    out_group(1).start()
    for off in range(1, chain):
        bias_copy(off).start()

    def both_ways(step, act):
        for way in (0, 1):
            there = a - step if way == 0 else a + step

            @pl.when((there >= 0) & (there < chain))
            def _(way=way, there=there):
                act(way, jnp.clip(there, 0, chain - 1))

    def weights_pass(way, row):
        for i in (1, 2):
            weight_copy(i, row, way).wait_recv()

            @pl.when(can(way))
            def _(i=i):
                weight_copy(i, row, way).start()

            group_copy(0, i, row).start()
            group_copy(1, i, row).start()

    def weights_side(way, row):
        for i in (1, 2):
            group_copy(0, i, row, arriving=True).wait_recv()
            group_copy(2, i, row).start()

    both_ways(1, weights_pass)

    def flip(c, _):
        rows = span(c, CHUNK)
        for h in range(heads):
            vt_ref[h, :, rows] = v_ref[h, rows, :].astype(F32).T.astype(BF)
        return 0

    lax.fori_loop(0, n * share // CHUNK, flip, 0)

    def own_copy(target, source):
        return remote(
            att_ref.at[span(target, share)],
            owned.at[source],
            ssa.at[target],
            rsa.at[source],
            (dp, target // cols, lax.rem(target, cols)),
        )

    def attend(c, _):
        attend_chunk(c, heads, q_ref, k_ref, v_ref, vt_ref, self_ref, att_ref, lse_ref)

        def send(target, _):
            end = (target + 1) * share

            @pl.when((end <= (c + 1) * CHUNK) & (end > c * CHUNK) & (target != me))
            def _():
                own_copy(target, me).start()

            return 0

        lax.fori_loop(0, n, send, 0)

        @pl.when(c == 0)
        def _():
            out_group(0, arriving=True).wait_recv()
            out_group(2).start()

        @pl.when(c > 0)
        def _():
            both_ways(c + 1, weights_pass)
            both_ways(c, weights_side)

        return 0

    lax.fori_loop(0, n * share // CHUNK, attend, 0)
    owned[me] = att_ref[span(me, share), :]
    for off in range(1, cols):
        pair_copy(1, off).start()
    pair_stay[1].start()
    for kind in (1, 2):
        out_group(kind, arriving=True).wait_recv()
    keep_out = pltpu.make_async_copy(outs_ref, outs_out, local_sem.at[3])
    keep_out.start()

    def collect(other, _):
        @pl.when(other != me)
        def _():
            own_copy(other, me).wait_send()
            own_copy(me, other).wait_recv()

        return 0

    lax.fori_loop(0, n, collect, 0)
    hidden_ref[...] = tokens_ref[...].astype(F32) + out_bias_ref[:1]

    def out_project(m, _):
        hidden_ref[...] += dot(owned[m], outs_ref[m])
        return 0

    lax.fori_loop(0, n, out_project, 0)

    def norm_two(i, _):
        cut = span(i, 16)
        two[cut, :] = layer_norm(hidden_ref[cut, :], gain_ref[1:], shift_ref[1:]).astype(BF)
        return 0

    lax.fori_loop(0, share // 16, norm_two, 0)
    for off in range(1, cols):
        pair_copy(0, off).start()
    pair_stay[0].start()
    both_ways(chain - 1, weights_side)
    owned_ref[...] = owned[...]
    for off in range(1, cols):
        for i in (0, 1):
            pair_copy(i, off).wait_send()
            pair_copy(i, off).wait_recv()
    for copy in pair_stay:
        copy.wait()
    keep_out.wait()
    keep.wait()
    keep_peers.wait()
    for off in range(1, cols):
        for copy in peer_copies(off):
            copy.wait_send()
    for i in (0, 1, 3):
        stay[i].wait()
    for off in range(1, chain):
        bias_copy(off).wait_send()
        bias_copy(off, arriving=True).wait_recv()
    for kind in range(3):
        out_group(kind).wait_send()

    def drain(row, _):
        for off in range(1, cols):
            cross_copy(row, off).wait_send()
            out_cross(row * cols + b, off).wait_send()

        @pl.when((row <= a) & (a < chain - 1))
        def _():
            chain_copy(row, 0).wait_send()
            for i in range(3):
                weight_copy(i, row, 0).wait_send()

        @pl.when((row >= a) & (a > 0))
        def _():
            chain_copy(row, 1).wait_send()
            for i in range(3):
                weight_copy(i, row, 1).wait_send()

        @pl.when(row != a)
        def _():
            for i in (1, 2):
                for kind in range(3):
                    group_copy(kind, i, row).wait_send()
                    if kind > 0:
                        group_copy(kind, i, row, arriving=True).wait_recv()

        return 0

    lax.fori_loop(0, chain, drain, 0)


def front(
    n, image_ids, lengths, tokens, cotangent, gain, shift, out_biases, w_qkv, bias_query, bias_value, w_up, w_down,
    w_out, bias_up,
):
    chain, cols = mp_parts(n)
    share, model = tokens.shape
    width = w_qkv.shape[2]
    heads = width // HEAD_DIM
    hidden = w_up.shape[1]
    rows = n * share
    vmem = pl.BlockSpec(memory_space=pltpu.VMEM)
    anywhere = pl.BlockSpec(memory_space=pl.ANY)
    ext = jax.ShapeDtypeStruct((heads, rows, LANES), BF)
    dma = pltpu.SemaphoreType.DMA
    return pl.pallas_call(
        functools.partial(front_kernel, n),
        name="front",
        out_shape=(
            jax.ShapeDtypeStruct((chain, share, model), BF),
            ext,
            ext,
            ext,
            jax.ShapeDtypeStruct((heads, 8, rows), F32),
            jax.ShapeDtypeStruct((rows, width), BF),
            jax.ShapeDtypeStruct((n, share, width), BF),
            jax.ShapeDtypeStruct((model, chain * hidden), BF),
            jax.ShapeDtypeStruct((chain * hidden, model), BF),
            jax.ShapeDtypeStruct((n, width, model), BF),
            jax.ShapeDtypeStruct((chain, 8, hidden), F32),
            jax.ShapeDtypeStruct((cols - 1,) + w_qkv.shape, BF),
            jax.ShapeDtypeStruct((8, rows), F32),
            jax.ShapeDtypeStruct((share, model), F32),
            jax.ShapeDtypeStruct((cols, share, model), BF),
            jax.ShapeDtypeStruct((cols, share, model), BF),
        ),
        in_specs=[pl.BlockSpec(memory_space=pltpu.SMEM)] * 2 + [vmem] * 11,
        out_specs=(anywhere,) + (vmem,) * 6 + (anywhere,) * 5 + (vmem,) * 2 + (anywhere,) * 2,
        scratch_shapes=[
            pltpu.VMEM((chain, share, model), BF),
            pltpu.VMEM((n, width, model), BF),
            pltpu.VMEM((share, model), BF),
            pltpu.VMEM((share, model), BF),
            pltpu.VMEM((cols - 1,) + w_qkv.shape, BF),
            pltpu.VMEM((cols - 1, 2, 8, width), F32),
            pltpu.VMEM((cols - 1, chain, 3, share, width), BF),
            pltpu.VMEM((cols - 1, chain, 3, share, width), BF),
            pltpu.VMEM((heads, LANES, rows), BF),
            pltpu.VMEM((n, share, width), BF),
            dma((2, chain)),
            dma((2, chain)),
            dma((cols, chain)),
            dma((cols, chain)),
            dma((cols,)),
            dma((cols,)),
            dma((cols,)),
            dma((cols,)),
            dma((n,)),
            dma((n,)),
            dma((3, 2, chain)),
            dma((3, 2, chain)),
            dma((cols, chain)),
            dma((cols, chain)),
            dma((3, 2, chain)),
            dma((3, 2, chain)),
            dma((3,)),
            dma((3,)),
            dma((chain,)),
            dma((chain,)),
            dma((2, cols)),
            dma((2, cols)),
            dma((8,)),
        ],
        compiler_params=pltpu.CompilerParams(
            collective_id=0, has_side_effects=True, vmem_limit_bytes=VMEM_BYTES
        ),
    )(
        image_ids,
        lengths,
        tokens,
        cotangent,
        gain,
        shift,
        out_biases,
        w_qkv,
        jnp.broadcast_to(jnp.stack([bias_query, bias_value])[:, None, :], (2, 8, width)),
        w_up,
        w_down,
        w_out,
        jnp.broadcast_to(bias_up[None, :], (8, hidden)),
    )


def attend_back_chunk(
    c, heads, q_ref, k_ref, v_ref, kt_ref, lse_ref, self_ref, att_ref, grad_ref, gq_ref, dk_ref, dv_ref
):
    rows = pl.ds(pl.multiple_of(c * CHUNK, CHUNK), CHUNK)
    grads = grad_ref[rows, :].astype(F32)
    products = grads * att_ref[rows, :].astype(F32)
    outs = []
    for h in range(heads):
        cut = slice(h * HEAD_DIM, (h + 1) * HEAD_DIM)
        inner = jnp.sum(products[:, cut], axis=1, keepdims=True)
        parts = split_three(-inner)
        lane = lax.broadcasted_iota(jnp.int32, (CHUNK, LANES - HEAD_DIM), 1)
        tail = jnp.zeros((CHUNK, LANES - HEAD_DIM), F32)
        for i, part in enumerate(parts):
            tail = jnp.where(lane == i, part.astype(F32), tail)
        grad_ext = jnp.concatenate([grads[:, cut], tail], axis=1).astype(BF)
        query = q_ref[h, rows, :]
        key_own = k_ref[h, rows, :]
        scores = dot(k_ref[h], query, NT)
        lse = lse_ref[h, :1, rows]
        probs = jnp.exp(scores - lse)
        shifted = dot(v_ref[h], grad_ext, NT)
        own = column_sum(query[:, :HEAD_DIM].astype(F32) * key_own[:, :HEAD_DIM].astype(F32))
        own_prob = jnp.exp(own + self_ref[:, rows] - lse)
        own_shifted = column_sum(v_ref[h, rows, :].astype(F32) * grad_ext.astype(F32))
        lower = lax.broadcasted_iota(jnp.int32, (8, CHUNK), 0) < 4
        both = jnp.where(lower, own_prob, own_prob * own_shifted).T
        own_prob, own_score = both[:, :1], both[:, 4:5]
        grad_scores = (probs * shifted).astype(BF)
        dv = dot(probs.astype(BF), grad_ext)
        dk = dot(grad_scores, query)
        dq = dot(kt_ref[h], grad_scores).T
        dq = (dq + own_score * key_own.astype(F32)) * SCALE
        outs.append(dq[:, :HEAD_DIM])

        @pl.when(c == 0)
        def _(h=h, dv=dv, dk=dk):
            dv_ref[h] = dv
            dk_ref[h] = dk

        @pl.when(c > 0)
        def _(h=h, dv=dv, dk=dk):
            dv_ref[h] += dv
            dk_ref[h] += dk

        dv_ref[h, rows, :] += own_prob * grad_ext.astype(F32)
        dk_ref[h, rows, :] += own_score * query.astype(F32)
    stacked = jnp.concatenate(outs, axis=1) if heads > 1 else outs[0]
    gq_ref[rows, :] = stacked.astype(BF)


REAR_REFS = (
    "gatt",
    "q",
    "k",
    "v",
    "lse",
    "self_bias",
    "att",
    "w",
    "peer_w",
    "normed",
    "tokens",
    "grad_hidden",
    "gain",
    "early",
    "up",
    "down",
    "out",
    "up_sum",
    "head_sum",
    "bias_out",
    "input_grad",
    "small_out",
    "grad",
    "kt",
    "dk",
    "dv",
    "gq",
    "gk",
    "gv",
    "kept",
    "pool_core",
    "pool_side",
    "way_in",
    "done",
    "out_in",
    "local",
    "local_in",
    "local_side",
    "local_done",
    "acc",
    "peer_in",
    "peer_acc",
    "peer_got",
    "way_gn",
    "gn",
    "small",
    "small_in",
    "bias_sum",
    "bias_in",
    "sa",
    "ra",
    "so",
    "ro",
    "sc",
    "rc",
    "sk",
    "ss",
    "rs",
    "sz",
    "rz",
    "sg",
    "rg",
    "st",
    "rt",
    "sy",
    "ry",
    "sh",
    "rh",
    "sx",
    "rx",
    "sw",
    "rw",
    "sn",
    "rn",
    "sm",
    "rm",
    "sb",
    "rb",
    "sl",
)


def rear_kernel(n, *refs):
    r = types.SimpleNamespace(**dict(zip(REAR_REFS, refs)))
    chain, cols = mp_parts(n)
    heads, total, _ = r.q.shape
    _, share, width = r.gatt.shape
    model = r.w.shape[1]
    hidden = r.up.shape[0] // chain
    rows = hidden // PARTS
    dg, dp = lax.axis_index("dg"), lax.axis_index("dp")
    a, b = lax.axis_index("mz"), lax.axis_index("mx")
    me = a * cols + b
    part = lax.rem(dp, PARTS)
    core_dp = dp + 1 - 2 * lax.rem(dp, 2)
    side_dp = dp + 2 - 4 * lax.rem(dp // 2, 2)
    core_part, side_part = lax.rem(core_dp, PARTS), lax.rem(side_dp, PARTS)
    far_part = PARTS - 1 - part
    core_id, side_id = (core_dp, a, b), (side_dp, a, b)
    far_id = (PARTS - 1 - dp, a, b)

    def mp_id(index):
        return dp, index // cols, lax.rem(index, cols)

    barrier = pltpu.get_barrier_semaphore()
    for off in range(1, n):
        pl.semaphore_signal(
            barrier, inc=1, device_id=(dg,) + mp_id(lax.rem(me + off, n)), device_id_type=MESH
        )
    for peer in (core_id, side_id, far_id):
        pl.semaphore_signal(barrier, inc=1, device_id=(dg,) + peer, device_id_type=MESH)
    pl.semaphore_wait(barrier, n + 2)

    def remote(src, dst, send, recv, device):
        return pltpu.make_async_remote_copy(
            src_ref=src,
            dst_ref=dst,
            send_sem=send,
            recv_sem=recv,
            device_id=(dg,) + device,
            device_id_type=MESH,
        )

    def span(index, size):
        return pl.ds(pl.multiple_of(index * size, size), size)

    def in_order(i):
        near = jnp.where(2 * a < chain, 1, 0)
        return jnp.where(lax.rem(i, 2) == near, i // 2, chain - 1 - i // 2)

    def first_service(t):
        return chain - 1 - jnp.maximum(t, chain - 1 - t)

    def add_rows(dst, *terms):
        count = dst.shape[0]
        step = 32 if count % 32 == 0 else 16

        def one(i, _):
            cut = span(i, step)
            value = terms[0][cut, :].astype(F32)
            for term in terms[1:]:
                value = value + term[cut, :].astype(F32)
            dst[cut, :] = value.astype(dst.dtype)
            return 0

        lax.fori_loop(0, count // step, one, 0)

    def loop(count, act):
        def one(i, _):
            act(i)
            return 0

        lax.fori_loop(0, count, one, 0)

    def others(act):
        def one(m):
            @pl.when(m != me)
            def _():
                act(m)

        loop(n, one)

    def row_copy(target, source):
        return remote(
            r.gatt.at[target], r.grad.at[span(source, share)], r.sa.at[target], r.ra.at[source], mp_id(target)
        )

    def out_copy(target, source):
        return remote(r.out.at[target], r.out_in.at[source], r.so.at[target], r.ro.at[source], mp_id(target))

    def source_rows(i, t, which):
        return (r.up, r.down)[i].at[span(t * PARTS + which, rows)]

    def core_copy(t, slot, i):
        return remote(
            source_rows(i, t, far_part if slot else core_part),
            r.pool_core.at[span((t * 2 + slot) * 2 + i, rows)],
            r.sc.at[t, slot, i],
            r.rc.at[t, slot, i],
            core_id,
        )

    def keep_copy(t, slot, i):
        return pltpu.make_async_copy(
            source_rows(i, t, side_part if slot else part),
            r.kept.at[t, slot, pl.ds(i * rows, rows)],
            r.sk.at[t, slot, i],
        )

    def side_copy(t):
        return remote(r.kept.at[t, 1], r.pool_side.at[span(t, 2 * rows)], r.ss.at[t], r.rs.at[t], side_id)

    def chain_id(way):
        return dp, jnp.clip(a + (1 if way == 0 else -1), 0, chain - 1), b

    def hop_of(way):
        return a if way == 0 else chain - 1 - a

    def ahead(way, t):
        return (t > a) if way == 0 else (t < a)

    def chain_copy(flow, way, t, fresh=False):
        own, inbox, send, recv = flow
        spot = inbox.at[way, t]
        return remote(own(t) if fresh else spot, spot, send.at[way, t], recv.at[way, t], chain_id(way))

    def chain_service(flow, s, prepare):
        own, inbox = flow[:2]

        def one(i):
            t = in_order(i)

            @pl.when(s == first_service(t))
            def _():
                prepare(t)

            for way in (0, 1):
                hop = hop_of(way)
                active = ahead(way, t) & (s == first_service(t) + hop)

                @pl.when(active & (hop == 0))
                def _(way=way):
                    chain_copy(flow, way, t, fresh=True).start()

                @pl.when(active & (hop > 0))
                def _(way=way):
                    chain_copy(flow, way, t).wait_recv()
                    add_rows(inbox.at[way, t], inbox.at[way, t], own(t))
                    chain_copy(flow, way, t).start()

        loop(chain, one)

    def chain_finish(flow, dst):
        own, inbox = flow[:2]

        @pl.when(a > 0)
        def _():
            chain_copy(flow, 0, a).wait_recv()

        @pl.when(a < chain - 1)
        def _():
            chain_copy(flow, 1, a).wait_recv()

        @pl.when((a > 0) & (a < chain - 1))
        def _():
            add_rows(dst, own(a), inbox.at[0, a], inbox.at[1, a])

        @pl.when(a == 0)
        def _():
            add_rows(dst, own(a), inbox.at[1, a])

        @pl.when(a == chain - 1)
        def _():
            add_rows(dst, own(a), inbox.at[0, a])

    def chain_drain(flow):
        def one(t):
            for way in (0, 1):

                @pl.when(ahead(way, t))
                def _(way=way):
                    chain_copy(flow, way, t).wait_send()

        loop(chain, one)

    def share_copy(share_flow, kind, arriving=False):
        own, everyone, send, recv = share_flow
        sent = side_part if kind == 2 else part
        got = (side_part, core_part, far_part)[kind]
        spot = everyone.at[got if arriving else sent]
        src = spot if kind == 2 or arriving else own
        return remote(src, spot, send.at[kind], recv.at[kind], side_id if kind == 0 else core_id)

    weights = (lambda t: r.kept.at[t, 0], r.way_in, r.sz, r.rz)
    grads = (lambda t: r.pool_side.at[span(t, share)], r.way_gn, r.sn, r.rn)
    share_weights = (r.done, r.up_sum, r.sg, r.rg)
    share_local = (r.local_done, r.head_sum, r.sh, r.rh)

    def small_peers(stage):
        if stage == 0:
            return [core_id, side_id, far_id]
        if stage == 1:
            return [(dp, a, lax.rem(b + off, cols)) for off in range(1, cols)]
        return [(dp, lax.rem(a + off, chain), b) for off in range(1, chain)]

    def small_copies(which, stage):
        src = r.early if which == 0 and stage == 0 else r.small.at[which, stage]
        return [
            remote(src, r.small_in.at[which, stage, i], r.sm.at[which, stage, i], r.rm.at[which, stage, i], peer)
            for i, peer in enumerate(small_peers(stage))
        ]

    def small_start(which, stage):
        for copy in small_copies(which, stage):
            copy.start()

    def small_sum(which, stage):
        value = r.early[...] if which == 0 and stage == 0 else r.small[which, stage]
        for i, copy in enumerate(small_copies(which, stage)):
            copy.wait_recv()
            value = value + r.small_in[which, stage, i]
        if stage < 2:
            r.small[which, stage + 1] = value
            small_start(which, stage + 1)
        else:
            r.small_out[which] = value

    def bias_copy(stage):
        return remote(
            r.bias_sum.at[stage], r.bias_in.at[stage], r.sb.at[stage], r.rb.at[stage], (core_id, side_id)[stage]
        )

    others(lambda m: row_copy(m, me).start())
    small_start(0, 0)

    def start_core(i):
        t = in_order(i)
        for slot in (1, 0):
            for k in (0, 1):
                core_copy(t, slot, k).start()
                keep_copy(t, slot, k).start()

    loop(chain, start_core)
    others(lambda m: out_copy(m, me).start())
    out_keep = pltpu.make_async_copy(r.out.at[me], r.out_in.at[me], r.sl.at[0])
    out_keep.start()
    r.grad[span(me, share), :] = r.gatt[me]

    def flip(c):
        cut = span(c, CHUNK)
        for h in range(heads):
            r.kt[h, :, cut] = r.k[h, cut, :].astype(F32).T.astype(BF)

    loop(total // CHUNK, flip)

    def core_sum(i):
        t = in_order(i)
        for slot in (1, 0):
            for k in (0, 1):
                keep_copy(t, slot, k).wait()
                core_copy(t, slot, k).wait_recv()
            add_rows(r.kept.at[t, slot], r.kept.at[t, slot], r.pool_core.at[span(t * 2 + slot, 2 * rows)])
            if slot == 1:
                side_copy(t).start()

    loop(chain, core_sum)
    others(lambda m: row_copy(me, m).wait_recv())

    def side_sum(t):
        side_copy(t).wait_recv()
        add_rows(r.kept.at[t, 0], r.kept.at[t, 0], r.pool_side.at[span(t, 2 * rows)])

    def cross_copy(k, lag, t):
        return remote(
            (r.gq, r.gk, r.gv)[k].at[span(t * cols + lax.rem(b + lag, cols), share)],
            r.peer_in.at[lag - 1, k, t],
            r.sx.at[k, lag, t],
            r.rx.at[k, lag, t],
            (dp, a, lax.rem(b + lag, cols)),
        )

    def attend(c):
        attend_back_chunk(
            c, heads, r.q, r.k, r.v, r.kt, r.lse, r.self_bias, r.att, r.grad, r.gq, r.dk, r.dv
        )

        def send(t):
            for lag in range(1, cols):
                end = (t * cols + lax.rem(b + lag, cols) + 1) * share

                @pl.when((end <= (c + 1) * CHUNK) & (end > c * CHUNK))
                def _(lag=lag):
                    cross_copy(0, lag, t).start()

        loop(chain, send)
        chain_service(weights, c, side_sum)

    loop(total // CHUNK, attend)

    def finish(c):
        cut = span(c, CHUNK)
        for src, dst in ((r.dk, r.gk), (r.dv, r.gv)):
            parts = [src[h, cut, :HEAD_DIM] for h in range(heads)]
            dst[cut, :] = (jnp.concatenate(parts, axis=1) if heads > 1 else parts[0]).astype(BF)

    loop(total // CHUNK, finish)

    def send_rest(i):
        for k in (1, 2):
            for lag in range(1, cols):
                cross_copy(k, lag, in_order(i)).start()

    loop(chain, send_rest)

    small_sum(0, 0)

    def partial_rows(t):
        cut = span(t * cols + b, share)
        value = dot(r.gq[cut, :], r.w[0], NT) + dot(r.gk[cut, :], r.w[1], NT)
        value = value + dot(r.gv[cut, :], r.w[2], NT)
        for slot in range(cols - 1):
            for k in range(3):
                value = value + dot(r.peer_in[slot, k, t], r.peer_w[slot, k], NT)
        return value.astype(BF)

    def bias_rows(c):
        ones = jnp.ones((8, CHUNK), BF)
        for t, src in ((0, r.gq), (1, r.gv)):
            value = dot(ones, src[span(c, CHUNK), :])

            @pl.when(c == 0)
            def _(t=t, value=value):
                r.bias_sum[0, t] = value

            @pl.when(c > 0)
            def _(t=t, value=value):
                r.bias_sum[0, t] += value

    loop(total // CHUNK, bias_rows)
    bias_copy(0).start()

    def head_grads(rows_of):
        def one(t):
            for k in range(3):
                value = dot(rows_of(k, t), r.normed[t], TN)

                @pl.when(t == 0)
                def _(k=k, value=value):
                    r.acc[k] = value

                @pl.when(t > 0)
                def _(k=k, value=value):
                    r.acc[k] += value

        loop(chain, one)

    def head_copy(off):
        return remote(
            r.peer_acc.at[off - 1],
            r.peer_got.at[off - 1],
            r.sw.at[off],
            r.rw.at[off],
            (dp, a, lax.rem(b - off + cols, cols)),
        )

    def cross_sum(t):
        for k in range(3):
            for lag in range(1, cols):
                cross_copy(k, lag, t).wait_recv()
        own = grads[0](t)
        own[...] = partial_rows(t)

    chain_service(grads, 0, cross_sum)
    chain_finish(weights, r.done)
    for kind in (0, 1):
        share_copy(share_weights, kind).start()
    weights_keep = pltpu.make_async_copy(r.done, r.up_sum.at[part], r.sl.at[1])
    weights_keep.start()
    chain_service(grads, 1, cross_sum)
    for off in range(1, cols):
        head_grads(lambda k, t: r.peer_in[off - 1, k, t])
        r.peer_acc[off - 1] = r.acc[...].astype(BF)
        head_copy(off).start()
    head_grads(lambda k, t: (r.gq, r.gk, r.gv)[k][span(t * cols + b, share), :])
    out_keep.wait()
    others(lambda m: out_copy(me, m).wait_recv())
    add_rows(r.local.at[0], *[r.out_in.at[m] for m in range(n)])

    def later(s, _):
        chain_service(grads, s, cross_sum)
        return 0

    lax.fori_loop(2, chain - 1, later, 0)
    for k in range(3):
        total_k = r.acc[k]
        for off in range(1, cols):
            if k == 0:
                head_copy(off).wait_recv()
            total_k = total_k + r.peer_got[off - 1, k].astype(F32)
        r.local[1 + k] = total_k.astype(BF)

    def local_core(slot):
        return remote(
            r.local.at[far_part if slot else core_part], r.local_in.at[slot], r.st.at[slot], r.rt.at[slot], core_id
        )

    local_side = remote(r.local.at[side_part], r.local_side, r.sy.at[0], r.ry.at[0], side_id)
    for slot in (1, 0):
        local_core(slot).start()
    small_sum(0, 1)
    for slot in (1, 0):
        local_core(slot).wait_recv()
        spot = r.local.at[side_part if slot else part]
        add_rows(spot, spot, r.local_in.at[slot])
        if slot == 1:
            local_side.start()
    bias_copy(0).wait_recv()
    r.bias_sum[1] = r.bias_sum[0] + r.bias_in[0]
    bias_copy(1).start()
    share_copy(share_weights, 0, arriving=True).wait_recv()
    share_copy(share_weights, 2).start()
    local_side.wait_recv()
    bias_copy(1).wait_recv()
    r.bias_out[...] = r.bias_sum[1] + r.bias_in[1]
    add_rows(r.local_done, r.local.at[part], r.local_side)
    for kind in (0, 1):
        share_copy(share_local, kind).start()
    local_keep = pltpu.make_async_copy(r.local_done, r.head_sum.at[part], r.sl.at[2])
    local_keep.start()
    chain_finish(grads, r.gn)
    step = 32 if share % 32 == 0 else 16

    def norm_back(i, sums):
        cut = span(i, step)
        values = r.tokens[cut, :].astype(F32)
        grad = r.gn[cut, :]
        centered = values - jnp.mean(values, axis=-1, keepdims=True)
        scale = lax.rsqrt(jnp.mean(centered * centered, axis=-1, keepdims=True) + epsilon)
        unit = centered * scale
        scaled = grad * r.gain[...]
        along = jnp.mean(scaled * unit, axis=-1, keepdims=True)
        back = (scaled - jnp.mean(scaled, axis=-1, keepdims=True) - unit * along) * scale
        r.input_grad[cut, :] = (r.grad_hidden[cut, :] + back).astype(BF)
        gains = jnp.sum(grad * unit, axis=0, keepdims=True)
        return sums[0] + gains, sums[1] + jnp.sum(grad, axis=0, keepdims=True)

    zero = jnp.zeros((1, model), F32)
    gains, shifts = lax.fori_loop(0, share // step, norm_back, (zero, zero))
    upper = lax.broadcasted_iota(jnp.int32, (8, model), 0) == 0
    r.small[1, 0] = jnp.where(upper, gains, shifts)
    small_start(1, 0)
    small_sum(0, 2)
    share_copy(share_local, 0, arriving=True).wait_recv()
    share_copy(share_local, 2).start()
    for stage in range(3):
        small_sum(1, stage)

    weights_keep.wait()
    local_keep.wait()
    for flow in (share_weights, share_local):
        for kind in range(3):
            share_copy(flow, kind).wait_send()
            if kind > 0:
                share_copy(flow, kind, arriving=True).wait_recv()
    for slot in (1, 0):
        local_core(slot).wait_send()
    local_side.wait_send()
    for off in range(1, cols):
        head_copy(off).wait_send()
    for stage in range(2):
        bias_copy(stage).wait_send()
    for which in range(2):
        for stage in range(3):
            for copy in small_copies(which, stage):
                copy.wait_send()
    others(lambda m: row_copy(m, me).wait_send())
    others(lambda m: out_copy(m, me).wait_send())
    chain_drain(weights)
    chain_drain(grads)

    def drain(t):
        side_copy(t).wait_send()
        for slot in (1, 0):
            for k in (0, 1):
                core_copy(t, slot, k).wait_send()
        for lag in range(1, cols):
            for k in range(3):
                cross_copy(k, lag, t).wait_send()

    loop(chain, drain)


def rear(
    n, grad_rows, q_ext, k_ext, v_ext, lse, self_bias, attended, w_qkv, peer_w, normed, tokens, grad_hidden, gain,
    early, grad_up, grad_down, grad_out,
):
    chain, cols = mp_parts(n)
    heads, total, _ = q_ext.shape
    _, share, width = grad_rows.shape
    model = w_qkv.shape[1]
    rows = 2 * (grad_up.shape[0] // chain // PARTS)
    vmem = pl.BlockSpec(memory_space=pltpu.VMEM)
    anywhere = pl.BlockSpec(memory_space=pl.ANY)
    dma = pltpu.SemaphoreType.DMA
    head = pltpu.VMEM((total, width), BF)
    most = max(chain, cols, PARTS) - 1
    return pl.pallas_call(
        functools.partial(rear_kernel, n),
        name="rear",
        out_shape=(
            jax.ShapeDtypeStruct((PARTS, rows, model), BF),
            jax.ShapeDtypeStruct((PARTS, width, model), BF),
            jax.ShapeDtypeStruct((2, 8, width), F32),
            jax.ShapeDtypeStruct((share, model), BF),
            jax.ShapeDtypeStruct((2, 8, model), F32),
        ),
        in_specs=[vmem] * 14 + [anywhere] * 3,
        out_specs=(anywhere, anywhere, vmem, vmem, vmem),
        scratch_shapes=[
            head,
            pltpu.VMEM((heads, LANES, total), BF),
            pltpu.VMEM((heads, total, LANES), F32),
            pltpu.VMEM((heads, total, LANES), F32),
            head,
            head,
            head,
            pltpu.VMEM((chain, 2, rows, model), BF),
            pltpu.VMEM((chain * 2 * rows, model), BF),
            pltpu.VMEM((max(chain * rows, chain * share), model), BF),
            pltpu.VMEM((2, chain, rows, model), BF),
            pltpu.VMEM((rows, model), BF),
            pltpu.VMEM((n, width, model), BF),
            pltpu.VMEM((PARTS, width, model), BF),
            pltpu.VMEM((2, width, model), BF),
            pltpu.VMEM((width, model), BF),
            pltpu.VMEM((width, model), BF),
            pltpu.VMEM((3, width, model), F32),
            pltpu.VMEM((cols - 1, 3, chain, share, width), BF),
            pltpu.VMEM((cols - 1, 3, width, model), BF),
            pltpu.VMEM((cols - 1, 3, width, model), BF),
            pltpu.VMEM((2, chain, share, model), BF),
            pltpu.VMEM((share, model), F32),
            pltpu.VMEM((2, 3, 8, model), F32),
            pltpu.VMEM((2, 3, most, 8, model), F32),
            pltpu.VMEM((2, 2, 8, width), F32),
            pltpu.VMEM((2, 2, 8, width), F32),
            dma((n,)),
            dma((n,)),
            dma((n,)),
            dma((n,)),
            dma((chain, 2, 2)),
            dma((chain, 2, 2)),
            dma((chain, 2, 2)),
            dma((chain,)),
            dma((chain,)),
            dma((2, chain)),
            dma((2, chain)),
            dma((3,)),
            dma((3,)),
            dma((2,)),
            dma((2,)),
            dma((1,)),
            dma((1,)),
            dma((3,)),
            dma((3,)),
            dma((3, cols, chain)),
            dma((3, cols, chain)),
            dma((cols,)),
            dma((cols,)),
            dma((2, chain)),
            dma((2, chain)),
            dma((2, 3, most)),
            dma((2, 3, most)),
            dma((2,)),
            dma((2,)),
            dma((3,)),
        ],
        compiler_params=pltpu.CompilerParams(
            collective_id=1, has_side_effects=True, vmem_limit_bytes=VMEM_BYTES
        ),
    )(
        grad_rows, q_ext, k_ext, v_ext, lse, self_bias, attended, w_qkv, peer_w, normed, tokens, grad_hidden,
        gain[None, :], early, grad_up, grad_down, grad_out,
    )


def body(
    n,
    groups,
    tokens,
    image_ids,
    lengths,
    w_qkv,
    bias_query,
    bias_value,
    w_out,
    w_up,
    bias_up,
    w_down,
    out_biases,
    norm_gain,
    norm_bias,
    cotangent,
):
    share_rows = tokens.shape[0]
    a, b = lax.axis_index("mz"), lax.axis_index("mx")
    chain, cols = mp_parts(n)
    model_index = a * cols + b
    model, hidden = w_up.shape
    width = w_out.shape[0]

    def shifted(values, off):
        return lax.ppermute(values, "mx", [(i, (i + off) % cols) for i in range(cols)])

    def pair_sum(partial):
        blocks = jnp.split(partial, cols)
        total = blocks[0].astype(F32)
        for off in range(1, cols):
            total = total + shifted(blocks[off].astype(BF), cols - off).astype(F32)
        return total

    (
        gathered_one, q_ext, k_ext, v_ext, log_totals, attended, owned,
        up_all, down_all, out_all, bias_all, peer_w, self_bias, hidden_one, rows_two, grad_mlp,
    ) = front(
        n,
        image_ids,
        lengths,
        tokens,
        cotangent,
        norm_gain,
        norm_bias,
        out_biases,
        w_qkv,
        bias_query,
        bias_value,
        w_up,
        w_down,
        w_out,
        bias_up,
    )
    grad_out = grad_mlp[0].astype(F32)
    rows_two = rows_two.reshape(cols * share_rows, model)
    grad_mlp = grad_mlp.reshape(cols * share_rows, model)
    owned = jnp.transpose(owned, (1, 0, 2)).reshape(share_rows, -1)
    bias_all = bias_all[:, 0].reshape(-1)
    pre_act = jnp.dot(rows_two, up_all, preferred_element_type=F32) + bias_all
    activated = exact_gelu(pre_act).astype(BF)
    grad_act = jnp.einsum("rd,fd->rf", grad_mlp, down_all, preferred_element_type=F32)
    _, gelu_back = jax.vjp(exact_gelu, pre_act)
    grad_pre = gelu_back(grad_act)[0].astype(BF)
    grad_normed_two = pair_sum(jnp.einsum("rf,df->rd", grad_pre, up_all, preferred_element_type=F32))
    output_full = (
        hidden_one
        + pair_sum(jnp.dot(activated, down_all, preferred_element_type=F32))
        + out_biases[1]
    )
    grad_up_all = jnp.einsum("rf,rd->fd", grad_pre, rows_two, preferred_element_type=F32)
    grad_down_all = jnp.einsum("rf,rd->fd", activated, grad_mlp, preferred_element_type=F32)
    grad_bias_up = jnp.sum(grad_pre, axis=0, dtype=F32)

    _, norm_two_back = jax.vjp(layer_norm, hidden_one, norm_gain[1], norm_bias[1])
    grad_from_two, gain_two, shift_two = norm_two_back(grad_normed_two)
    grad_hidden = grad_out + grad_from_two
    grad_proj = grad_hidden.astype(BF)
    grad_w_out = jnp.einsum("re,rd->ed", owned, grad_proj, preferred_element_type=F32).astype(BF)
    grad_rows = jnp.einsum(
        "rd,ned->nre", grad_proj, out_all.reshape(n, width, model), preferred_element_type=F32
    ).astype(BF)
    bias_rows = lax.dynamic_update_slice(
        jnp.zeros((chain, cols, hidden), F32), grad_bias_up.reshape(chain, 1, hidden), (0, b, 0)
    )
    early = [gain_two, shift_two, jnp.sum(grad_hidden, axis=0), jnp.sum(grad_out, axis=0)]
    early = jnp.concatenate([jnp.stack(early), bias_rows.reshape(-1, model)])
    hidden_sum, head_sum, bias_sum, input_grad, small = rear(
        n,
        grad_rows,
        q_ext,
        k_ext,
        v_ext,
        log_totals,
        self_bias,
        attended,
        w_qkv,
        peer_w,
        gathered_one,
        tokens,
        grad_hidden,
        norm_gain[0],
        early,
        grad_up_all.astype(BF),
        grad_down_all.astype(BF),
        grad_w_out.reshape(n, width, model),
    )
    if groups > 1:
        hidden_sum, head_sum, bias_sum, small = lax.psum((hidden_sum, head_sum, bias_sum, small), "dg")
    half = hidden // PARTS
    grad_w_up = hidden_sum[:, :half].reshape(hidden, model).T.astype(F32)
    grad_w_down = hidden_sum[:, half:].reshape(hidden, model).astype(F32)
    grad_w_out = head_sum[0].astype(F32)
    grad_w_qkv = jnp.transpose(head_sum[1:], (0, 2, 1)).astype(F32)
    grad_bias_query, grad_bias_value = bias_sum[:, 0]
    grad_bias_up = lax.dynamic_slice_in_dim(
        small[0, 4:].reshape(-1), model_index * hidden, hidden, 0
    )
    return (
        output_full.astype(BF),
        input_grad,
        grad_w_qkv,
        grad_bias_query,
        grad_bias_value,
        grad_w_out,
        grad_w_up,
        grad_bias_up,
        grad_w_down,
        small[0, 2:4],
        jnp.stack([small[1, 0], small[0, 0]]),
        jnp.stack([small[1, 1], small[0, 1]]),
    )


def solution(mesh):
    n = mesh.shape["mp"]
    chain, cols = mp_parts(n)
    groups = mesh.shape["dp"] // PARTS
    dp, mp = ("dg", "dp"), ("mz", "mx")
    every = dp + mp
    split = jax.sharding.Mesh(mesh.devices.reshape(groups, PARTS, chain, cols), every)
    in_specs = (
        P(every, None),
        P(dp),
        P(dp, None),
        P(None, None, mp),
        P(mp),
        P(mp),
        P(mp, None),
        P(None, mp),
        P(mp),
        P(mp, None),
        P(),
        P(),
        P(),
        P(every, None),
    )
    out_specs = (
        P(every, None),
        P(every, None),
        P(None, None, mp),
        P(mp),
        P(mp),
        P(mp, None),
        P(None, mp),
        P(mp),
        P(mp, None),
        P(),
        P(),
        P(),
    )
    return jax.shard_map(
        functools.partial(body, n, groups),
        mesh=split,
        in_specs=in_specs,
        out_specs=out_specs,
        check_vma=False,
    )
```

profile of v0, /device:TPU:0, one launch (start us, length us, event | category | flops | bytes accessed | tf_op | source)
XLA Modules:
  0.0 356.0 jit_solution(9988874436422145564)
XLA Ops:
  0.6 0.7 pad_maximum_fusion.2
  1.3 1.3 broadcast_in_dim.11.bup_ref
  3.2 126.3 %front.1 = (bf16[4,288,1024]{2,1,0:T(8,128)(2,1)}, bf16[2,2304,128]{2,1,0:T(8,128)(2,1)}, bf16[2,2304,128]{2,1,0:T(8,128)(2,1)}, bf16[2,2304,128]{2,1,0:T(8,128)...) custom-call(s32[2304]{0:T(1024)} %ids_ref.1, ...), custom_call_target="tpu_custom_call" | custom-call | tf_op jit(solution)/shard_map/front/pallas_call | solution.py:627
  129.6 0.8 slice.50
  130.4 4.9 %fusion.24 = f32[576,2048]{1,0:T(8,128)S(1)} fusion(bf16[576,1024]{1,0:T(8,128)(2,1)} %bitcast.96, bf16[1024,2048]{1,0:T(8,128)(2,1)} %get-tuple-element.35), kind=kOutput, calls=%fused_computation.68 | convolution fusion | flops 2415919104 | bytes 10092544 | tf_op jit(solution)/shard_map/dot_general | solution.py:1483
  135.3 14.5 %convert_reduce_fusion = (f32[2048]{0:T(1024)}, bf16[576,2048]{1,0:T(8,128)(2,1)S(1)}, f32[576,2048]{1,0:T(8,128)S(1)}) fusion(f32[576,2048]{1,0:T(8,128)S(1)} %fusion.24, f32[2048]{0:T(1024)S(1)} %bitcast.85, bf16[576,1024]{1,0:T(8,128)(2,1)S(1)} %bitcast.79, bf16[2048,1024]{1,0:T(8,128)(2,1)S(1)} %copy-done.19), kind=kOutput, calls=%fused_computation.2 | convolution fusion | flops 2504390656 | bytes 17186816 | tf_op jit(solution)/shard_map/rd,fd->rf/dot_general | solution.py:1485
  149.8 1.2 multiply_convert_fusion
  151.1 2.6 fusion.25
  153.7 1.0 split.41
  154.7 1.4 collective-permute-start
  156.2 2.7 fusion.26
  158.9 0.9 split.40
  161.6 5.1 %convolution_convert_fusion.refs_15_ = bf16[2048,1024]{1,0:T(8,128)(2,1)} fusion(bf16[576,2048]{1,0:T(8,128)(2,1)S(1)} %multiply_convert_fusion, bf16[576,1024]{1,0:T(8,128)(2,1)S(1)} %bitcast.80), kind=kOutput, calls=%fused_computation.18 | convolution fusion | flops 2418016256 | bytes 7733248 | tf_op jit(solution)/shard_map/rf,rd->fd/dot_general | solution.py:1495
  168.9 0.7 dynamic_update_slice.3
  170.3 7.5 %convolution_convert_fusion.1.refs_14_ = bf16[2048,1024]{1,0:T(8,128)(2,1)} fusion(bf16[576,2048]{1,0:T(8,128)(2,1)} %copy-done.22, bf16[576,1024]{1,0:T(8,128)(2,1)} %bitcast.97), kind=kOutput, calls=%fused_computation.19 | convolution fusion | flops 2418016256 | bytes 7733248 | tf_op jit(solution)/shard_map/rf,rd->fd/dot_general | solution.py:1494
  177.9 1.2 collective-permute-done.1
  179.1 1.6 multiply_reduce_fusion
  180.7 2.7 fusion.21
  183.7 2.6 convolution_convert_fusion.2
  186.3 1.6 fusion.6.refs_0_
  188.6 149.6 %rear.1 = (bf16[4,256,1024]{2,1,0:T(8,128)(2,1)}, bf16[4,128,1024]{2,1,0:T(8,128)(2,1)}, f32[2,8,128]{2,1,0:T(8,128)}, bf16[288,1024]{1,0:T(8,128)(2,1)}, f32[2,8,1024]{2,1,0:T(8,128)}) custom-call(bf16[8,288,128]{2,1,0:T(8,128)(2,1)} %fusion.6.refs_0_, bf16[2,2304,128]{2,1,0:T(8,128)(2,1)} %get-tuple-element.40.refs_1_, ...), custom_call_target="tpu_custom_call" | custom-call | tf_op jit(solution)/shard_map/rear/pallas_call | solution.py:1343
  338.2 2.6 convert_bitcast_fusion
  340.8 1.8 bitcast_convert_fusion.2
  342.6 0.8 slice_bitcast_fusion.3
  343.5 0.8 slice_bitcast_fusion
  344.2 1.4 slice_bitcast_fusion.1
  345.8 1.9 bitcast_convert_fusion
  347.7 1.8 copy.29
  349.5 3.0 copy.30
  352.5 1.2 slice_bitcast_fusion.6
  353.7 0.7 dynamic_slice.3
  355.0 0.8 copy.42
  (65 shorter events, 7.1 us)
Async XLA Ops:
  130.4 4.9 %copy-start.5 = (bf16[2,288,1024]{2,1,0:T(8,128)(2,1)S(1)}, bf16[2,288,1024]{2,1,0:T(8,128)(2,1)}, u32[]{:S(2)}) copy-start(bf16[2,288,1024]{2,1,0:T(8,128)(2,1)} %get-tuple-element.39) | copy-start | bytes 3538948
  130.4 4.9 %copy-start.19 = (bf16[2048,1024]{1,0:T(8,128)(2,1)S(1)}, bf16[2048,1024]{1,0:T(8,128)(2,1)}, u32[]{:S(2)}) copy-start(bf16[2048,1024]{1,0:T(8,128)(2,1)} %get-tuple-element.37) | copy-start | bytes 12582916
  149.8 6.3 %copy-start.22 = (bf16[576,2048]{1,0:T(8,128)(2,1)}, bf16[576,2048]{1,0:T(8,128)(2,1)S(1)}, u32[]{:S(2)}) copy-start(bf16[576,2048]{1,0:T(8,128)(2,1)S(1)} %get-tuple-element.82) | copy-start | bytes 7077892
  151.0 5.1 %copy-start.18 = (bf16[1024,2048]{1,0:T(8,128)(2,1)S(1)}, bf16[1024,2048]{1,0:T(8,128)(2,1)}, u32[]{:S(2)}) copy-start(bf16[1024,2048]{1,0:T(8,128)(2,1)} %get-tuple-element.35) | copy-start | bytes 12582916
  153.7 2.4 copy-start.3
  154.7 26.0 %collective-permute-start = (bf16[288,1024]{1,0:T(8,128)(2,1)}, bf16[288,1024]{1,0:T(8,128)(2,1)}, u32[]{:S(2)}, u32[]{:S(2)}) collective-permute-start(bf16[288,1024]{1,0:T(8,128)(2,1)} %split.41), channel_id=1, source_target_pairs={{0,1},{1,0},{2,3},{3,2},{4,5},{5,4},{6,7},{7,6},{8,9},{9,8},{10,11... | collective-permute-start | bytes 1769480 | tf_op jit(solution)/shard_map/ppermute | solution.py:1449
  156.1 4.3 %copy-start.12 = (f32[2,1024]{1,0:T(2,128)S(1)}, f32[2,1024]{1,0:T(2,128)}, u32[]{:S(2)}) copy-start(f32[2,1024]{1,0:T(2,128)} %gain_ref.1) | copy-start | bytes 24580
  156.2 4.8 %copy-start.14 = (f32[2,1024]{1,0:T(2,128)S(1)}, f32[2,1024]{1,0:T(2,128)}, u32[]{:S(2)}) copy-start(f32[2,1024]{1,0:T(2,128)} %out_bias_ref.1) | copy-start | bytes 24580
  159.8 19.3 %collective-permute-start.1 = (bf16[288,1024]{1,0:T(8,128)(2,1)}, bf16[288,1024]{1,0:T(8,128)(2,1)}, u32[]{:S(2)}, u32[]{:S(2)}) collective-permute-start(bf16[288,1024]{1,0:T(8,128)(2,1)} %split.40), channel_id=1, source_target_pairs={{0,1},{1,0},{2,3},{3,2},{4,5},{5,4},{6,7},{7,6},{8,9},{9,8},{10,11... | collective-permute-start | bytes 1769480 | tf_op jit(solution)/shard_map/ppermute | solution.py:1449
  161.6 5.1 %copy-start = (f32[288,1024]{1,0:T(8,128)S(1)}, f32[288,1024]{1,0:T(8,128)}, u32[]{:S(2)}) copy-start(f32[288,1024]{1,0:T(8,128)} %get-tuple-element.33) | copy-start | bytes 3538948
  166.8 0.6 copy-start.10
  167.7 0.6 copy-start.15
  170.2 7.5 %copy-start.6 = (bf16[2,288,1024]{2,1,0:T(8,128)(2,1)S(1)}, bf16[2,288,1024]{2,1,0:T(8,128)(2,1)}, u32[]{:S(2)}) copy-start(bf16[2,288,1024]{2,1,0:T(8,128)(2,1)} %get-tuple-element.39) | copy-start | bytes 3538948
  170.2 8.8 %copy-start.9 = (f32[1,1024]{1,0:T(1,128)S(1)}, f32[1,1024]{1,0:T(1,128)}, u32[]{:S(2)}) copy-start(f32[1,1024]{1,0:T(1,128)} %get-tuple-element.98) | copy-start | bytes 12292
  170.2 8.8 %copy-start.11 = (f32[288]{0:T(512)S(1)}, f32[288]{0:T(512)}, u32[]{:S(2)}) copy-start(f32[288]{0:T(512)} %copy-done.10) | copy-start | bytes 3460
  170.2 8.8 %copy-start.13 = (f32[288]{0:T(512)S(1)}, f32[288]{0:T(512)}, u32[]{:S(2)}) copy-start(f32[288]{0:T(512)} %fusion.16) | copy-start | bytes 3460
  170.2 10.4 %copy-start.16 = (f32[288]{0:T(512)S(1)}, f32[288]{0:T(512)}, u32[]{:S(2)}) copy-start(f32[288]{0:T(512)} %copy-done.15) | copy-start | bytes 3460
  170.3 10.4 %copy-start.17 = (f32[1,1024]{1,0:T(1,128)S(1)}, f32[1,1024]{1,0:T(1,128)}, u32[]{:S(2)}) copy-start(f32[1,1024]{1,0:T(1,128)} %slice.51) | copy-start | bytes 12292
  177.8 2.9 copy-start.4
  180.7 3.0 copy-start.21
  183.4 2.9 copy-start.20
  183.7 2.7 copy-start.1
  183.7 4.3 %copy-start.8 = (f32[1,4,2,512]{3,1,2,0:T(4,128)S(1)}, f32[1,4,2,512]{3,1,2,0:T(4,128)}, u32[]{:S(2)}) copy-start(f32[1,4,2,512]{3,1,2,0:T(4,128)} %copy.32) | copy-start | bytes 49156
  338.2 7.4 %copy-start.2 = (bf16[4,256,1024]{2,1,0:T(8,128)(2,1)S(1)}, bf16[4,256,1024]{2,1,0:T(8,128)(2,1)}, u32[]{:S(2)}) copy-start(bf16[4,256,1024]{2,1,0:T(8,128)(2,1)} %get-tuple-element.52) | copy-start | bytes 6291460
  347.7 7.3 %copy-start.7 = (bf16[288,1024]{1,0:T(8,128)(2,1)S(1)}, bf16[288,1024]{1,0:T(8,128)(2,1)}, u32[]{:S(2)}) copy-start(bf16[288,1024]{1,0:T(8,128)(2,1)} %get-tuple-element.116) | copy-start | bytes 1769476
where the time goes:
time: 359 us; the launch traced here: 356 us
  Pallas kernels  276 us (77%)
  matrix products  41.5 us (12%)
  local copies, waits for them, and re-layouts  19.7 us (5%)
  other arithmetic  14.5 us (4%)
    pallas_call x1, Pallas kernels, rear(): pl.pallas_call(functools.partial(rear_kernel, n), name='rear', out_shape=...  150 us
    pallas_call x1, Pallas kernels, front(): pl.pallas_call(functools.partial(front_kernel, n), name='front', out_shap...  126 us
    dot_general x1, matrix products, body(): jnp.einsum('rd,fd->rf', grad_mlp, down_all, preferred_element_type=F32)  14.5 us
    dot_general x1, matrix products, body(): jnp.einsum('rf,rd->fd', grad_pre, rows_two, preferred_element_type=F32)  7.49 us
  transfers between devices with their start and end apart: 2, of which 1 were waited for; matrix products, arithmetic and copies ran while one was open for 6% of the time, Pallas kernels for 0%

commit v1 on v0

--- a/solution.py
+++ b/solution.py
@@ -787,15 +787,11 @@
     "pool_core",
     "pool_side",
     "way_in",
-    "done",
     "out_in",
-    "local",
     "local_in",
     "local_side",
-    "local_done",
     "acc",
     "peer_in",
-    "peer_acc",
     "peer_got",
     "way_gn",
     "gn",
@@ -843,7 +839,15 @@
     _, share, width = r.gatt.shape
     model = r.w.shape[1]
     hidden = r.up.shape[0] // chain
-    rows = hidden // PARTS
+    rows, out_rows = hidden // PARTS, width // PARTS
+    block_rows = 2 * rows + cols * out_rows
+    done_rows = 2 * rows + out_rows
+    local_rows = 3 * width // PARTS
+    head_base = (cols - 1) * 3 * width
+    done_base = head_base + 3 * width
+    local = r.pool_core.at[pl.ds(head_base, 3 * width)]
+    done = r.pool_core.at[pl.ds(done_base, block_rows)]
+    local_done = r.pool_core.at[pl.ds(done_base + block_rows, local_rows)]
     dg, dp = lax.axis_index("dg"), lax.axis_index("dp")
     a, b = lax.axis_index("mz"), lax.axis_index("mx")
     me = a * cols + b
@@ -881,11 +885,9 @@
         return pl.ds(pl.multiple_of(index * size, size), size)
 
     def in_order(i):
-        near = jnp.where(2 * a < chain, 1, 0)
-        return jnp.where(lax.rem(i, 2) == near, i // 2, chain - 1 - i // 2)
-
-    def first_service(t):
-        return chain - 1 - jnp.maximum(t, chain - 1 - t)
+        low = jnp.where(chain - 1 - i > a, chain - 1 - i, chain - 2 - i)
+        high = jnp.where(i < a, i, i + 1)
+        return jnp.where(i == chain - 1, a, jnp.where(2 * a < chain, low, high))
 
     def add_rows(dst, *terms):
         count = dst.shape[0]
@@ -921,30 +923,29 @@
             r.gatt.at[target], r.grad.at[span(source, share)], r.sa.at[target], r.ra.at[source], mp_id(target)
         )
 
-    def out_copy(target, source):
-        return remote(r.out.at[target], r.out_in.at[source], r.so.at[target], r.ro.at[source], mp_id(target))
-
     def source_rows(i, t, which):
-        return (r.up, r.down)[i].at[span(t * PARTS + which, rows)]
+        if i < 2:
+            return (r.up, r.down)[i].at[span(t * PARTS + which, rows)]
+        return r.out.at[t * cols + lax.rem(b + i - 2, cols), span(which, out_rows)]
+
+    def offset(i):
+        return i * rows if i < 2 else 2 * rows + (i - 2) * out_rows
 
     def core_copy(t, slot, i):
+        src = source_rows(i, t, far_part if slot else core_part)
+        base = pl.multiple_of((t * 2 + slot) * block_rows + offset(i), 16)
         return remote(
-            source_rows(i, t, far_part if slot else core_part),
-            r.pool_core.at[span((t * 2 + slot) * 2 + i, rows)],
-            r.sc.at[t, slot, i],
-            r.rc.at[t, slot, i],
-            core_id,
+            src, r.pool_core.at[pl.ds(base, src.shape[0])], r.sc.at[t, slot, i], r.rc.at[t, slot, i], core_id
         )
 
     def keep_copy(t, slot, i):
+        src = source_rows(i, t, side_part if slot else part)
         return pltpu.make_async_copy(
-            source_rows(i, t, side_part if slot else part),
-            r.kept.at[t, slot, pl.ds(i * rows, rows)],
-            r.sk.at[t, slot, i],
+            src, r.kept.at[t, slot, pl.ds(offset(i), src.shape[0])], r.sk.at[t, slot, i]
         )
 
     def side_copy(t):
-        return remote(r.kept.at[t, 1], r.pool_side.at[span(t, 2 * rows)], r.ss.at[t], r.rs.at[t], side_id)
+        return remote(r.kept.at[t, 1], r.pool_side.at[span(t, block_rows)], r.ss.at[t], r.rs.at[t], side_id)
 
     def chain_id(way):
         return dp, jnp.clip(a + (1 if way == 0 else -1), 0, chain - 1), b
@@ -962,32 +963,29 @@
 
     def chain_service(flow, s, prepare):
         own, inbox = flow[:2]
-
-        def one(i):
-            t = in_order(i)
-
-            @pl.when(s == first_service(t))
-            def _():
+        for way in (0, 1):
+            hop = hop_of(way)
+            t = chain - 1 + a - s if way == 0 else s - hop
+            active = (t > a) & (t < chain) if way == 0 else (t >= 0) & (t < a)
+            spot = jnp.clip(t, 0, chain - 1)
+
+            @pl.when(active)
+            def _(way=way, t=spot):
                 prepare(t)
 
-            for way in (0, 1):
-                hop = hop_of(way)
-                active = ahead(way, t) & (s == first_service(t) + hop)
-
-                @pl.when(active & (hop == 0))
-                def _(way=way):
-                    chain_copy(flow, way, t, fresh=True).start()
-
-                @pl.when(active & (hop > 0))
-                def _(way=way):
-                    chain_copy(flow, way, t).wait_recv()
-                    add_rows(inbox.at[way, t], inbox.at[way, t], own(t))
-                    chain_copy(flow, way, t).start()
-
-        loop(chain, one)
-
-    def chain_finish(flow, dst):
+            @pl.when(active & (hop == 0))
+            def _(way=way, t=spot):
+                chain_copy(flow, way, t, fresh=True).start()
+
+            @pl.when(active & (hop > 0))
+            def _(way=way, t=spot):
+                chain_copy(flow, way, t).wait_recv()
+                add_rows(inbox.at[way, t], inbox.at[way, t], own(t))
+                chain_copy(flow, way, t).start()
+
+    def chain_finish(flow, dst, prepare):
         own, inbox = flow[:2]
+        prepare(a)
 
         @pl.when(a > 0)
         def _():
@@ -1029,8 +1027,8 @@
 
     weights = (lambda t: r.kept.at[t, 0], r.way_in, r.sz, r.rz)
     grads = (lambda t: r.pool_side.at[span(t, share)], r.way_gn, r.sn, r.rn)
-    share_weights = (r.done, r.up_sum, r.sg, r.rg)
-    share_local = (r.local_done, r.head_sum, r.sh, r.rh)
+    share_weights = (done.at[pl.ds(0, done_rows)], r.up_sum, r.sg, r.rg)
+    share_local = (local_done, r.head_sum, r.sh, r.rh)
 
     def small_peers(stage):
         if stage == 0:
@@ -1072,14 +1070,11 @@
     def start_core(i):
         t = in_order(i)
         for slot in (1, 0):
-            for k in (0, 1):
+            for k in range(2 + cols):
                 core_copy(t, slot, k).start()
                 keep_copy(t, slot, k).start()
 
     loop(chain, start_core)
-    others(lambda m: out_copy(m, me).start())
-    out_keep = pltpu.make_async_copy(r.out.at[me], r.out_in.at[me], r.sl.at[0])
-    out_keep.start()
     r.grad[span(me, share), :] = r.gatt[me]
 
     def flip(c):
@@ -1092,10 +1087,10 @@
     def core_sum(i):
         t = in_order(i)
         for slot in (1, 0):
-            for k in (0, 1):
+            for k in range(2 + cols):
                 keep_copy(t, slot, k).wait()
                 core_copy(t, slot, k).wait_recv()
-            add_rows(r.kept.at[t, slot], r.kept.at[t, slot], r.pool_core.at[span(t * 2 + slot, 2 * rows)])
+            add_rows(r.kept.at[t, slot], r.kept.at[t, slot], r.pool_core.at[span(t * 2 + slot, block_rows)])
             if slot == 1:
                 side_copy(t).start()
 
@@ -1104,7 +1099,7 @@
 
     def side_sum(t):
         side_copy(t).wait_recv()
-        add_rows(r.kept.at[t, 0], r.kept.at[t, 0], r.pool_side.at[span(t, 2 * rows)])
+        add_rows(r.kept.at[t, 0], r.kept.at[t, 0], r.pool_side.at[span(t, block_rows)])
 
     def cross_copy(k, lag, t):
         return remote(
@@ -1115,6 +1110,8 @@
             (dp, a, lax.rem(b + lag, cols)),
         )
 
+    chain_service(weights, 0, side_sum)
+
     def attend(c):
         attend_back_chunk(
             c, heads, r.q, r.k, r.v, r.kt, r.lse, r.self_bias, r.att, r.grad, r.gq, r.dk, r.dv
@@ -1129,7 +1126,11 @@
                     cross_copy(0, lag, t).start()
 
         loop(chain, send)
-        chain_service(weights, c, side_sum)
+
+        @pl.when(c < chain - 2)
+        def _():
+            chain_service(weights, c + 1, side_sum)
+
 
     loop(total // CHUNK, attend)
 
@@ -1147,6 +1148,18 @@
                 cross_copy(k, lag, in_order(i)).start()
 
     loop(chain, send_rest)
+    def out_copy(lag):
+        return remote(
+            done.at[pl.ds(offset(2 + lag), out_rows)],
+            r.out_in.at[lag - 1],
+            r.so.at[lag],
+            r.ro.at[lag],
+            (dp, a, lax.rem(b + lag, cols)),
+        )
+
+    chain_finish(weights, done, side_sum)
+    for lag in range(1, cols):
+        out_copy(lag).start()
 
     small_sum(0, 0)
 
@@ -1192,36 +1205,48 @@
 
     def head_copy(off):
         return remote(
-            r.peer_acc.at[off - 1],
+            r.pool_core.at[pl.ds((off - 1) * 3 * width, 3 * width)],
             r.peer_got.at[off - 1],
             r.sw.at[off],
             r.rw.at[off],
             (dp, a, lax.rem(b - off + cols, cols)),
         )
 
-    def cross_sum(t):
+    def cross_wait(t):
         for k in range(3):
             for lag in range(1, cols):
                 cross_copy(k, lag, t).wait_recv()
+
+    def cross_sum(t):
         own = grads[0](t)
         own[...] = partial_rows(t)
 
-    chain_service(grads, 0, cross_sum)
-    chain_finish(weights, r.done)
+    def first_sum(t):
+        cross_wait(t)
+        cross_sum(t)
+
+    def wait_rest(i):
+        @pl.when((i > 0) | ((a > 0) & (a < chain - 1)))
+        def _():
+            cross_wait(in_order(i))
+
+    chain_service(grads, 0, first_sum)
+    for lag in range(1, cols):
+        out_copy(lag).wait_recv()
+    spot = done.at[pl.ds(offset(2), out_rows)]
+    add_rows(spot, spot, *[r.out_in.at[lag - 1] for lag in range(1, cols)])
     for kind in (0, 1):
         share_copy(share_weights, kind).start()
-    weights_keep = pltpu.make_async_copy(r.done, r.up_sum.at[part], r.sl.at[1])
+    weights_keep = pltpu.make_async_copy(done.at[pl.ds(0, done_rows)], r.up_sum.at[part], r.sl.at[1])
     weights_keep.start()
+    loop(chain, wait_rest)
     chain_service(grads, 1, cross_sum)
     for off in range(1, cols):
         head_grads(lambda k, t: r.peer_in[off - 1, k, t])
-        r.peer_acc[off - 1] = r.acc[...].astype(BF)
+        for k in range(3):
+            r.pool_core[pl.ds(((off - 1) * 3 + k) * width, width), :] = r.acc[k].astype(BF)
         head_copy(off).start()
     head_grads(lambda k, t: (r.gq, r.gk, r.gv)[k][span(t * cols + b, share), :])
-    out_keep.wait()
-    others(lambda m: out_copy(me, m).wait_recv())
-    add_rows(r.local.at[0], *[r.out_in.at[m] for m in range(n)])
-
     def later(s, _):
         chain_service(grads, s, cross_sum)
         return 0
@@ -1232,21 +1257,21 @@
         for off in range(1, cols):
             if k == 0:
                 head_copy(off).wait_recv()
-            total_k = total_k + r.peer_got[off - 1, k].astype(F32)
-        r.local[1 + k] = total_k.astype(BF)
+            total_k = total_k + r.peer_got[off - 1, pl.ds(k * width, width)].astype(F32)
+        local[span(k, width), :] = total_k.astype(BF)
 
     def local_core(slot):
         return remote(
-            r.local.at[far_part if slot else core_part], r.local_in.at[slot], r.st.at[slot], r.rt.at[slot], core_id
-        )
-
-    local_side = remote(r.local.at[side_part], r.local_side, r.sy.at[0], r.ry.at[0], side_id)
+            local.at[span(far_part if slot else core_part, local_rows)], r.local_in.at[slot], r.st.at[slot], r.rt.at[slot], core_id
+        )
+
+    local_side = remote(local.at[span(side_part, local_rows)], r.local_side, r.sy.at[0], r.ry.at[0], side_id)
     for slot in (1, 0):
         local_core(slot).start()
     small_sum(0, 1)
     for slot in (1, 0):
         local_core(slot).wait_recv()
-        spot = r.local.at[side_part if slot else part]
+        spot = local.at[span(side_part if slot else part, local_rows)]
         add_rows(spot, spot, r.local_in.at[slot])
         if slot == 1:
             local_side.start()
@@ -1258,12 +1283,12 @@
     local_side.wait_recv()
     bias_copy(1).wait_recv()
     r.bias_out[...] = r.bias_sum[1] + r.bias_in[1]
-    add_rows(r.local_done, r.local.at[part], r.local_side)
+    add_rows(local_done, local.at[span(part, local_rows)], r.local_side)
     for kind in (0, 1):
         share_copy(share_local, kind).start()
-    local_keep = pltpu.make_async_copy(r.local_done, r.head_sum.at[part], r.sl.at[2])
+    local_keep = pltpu.make_async_copy(local_done, r.head_sum.at[part], r.sl.at[2])
     local_keep.start()
-    chain_finish(grads, r.gn)
+    chain_finish(grads, r.gn, cross_sum)
     step = 32 if share % 32 == 0 else 16
 
     def norm_back(i, sums):
@@ -1303,6 +1328,7 @@
     local_side.wait_send()
     for off in range(1, cols):
         head_copy(off).wait_send()
+        out_copy(off).wait_send()
     for stage in range(2):
         bias_copy(stage).wait_send()
     for which in range(2):
@@ -1310,14 +1336,13 @@
             for copy in small_copies(which, stage):
                 copy.wait_send()
     others(lambda m: row_copy(m, me).wait_send())
-    others(lambda m: out_copy(m, me).wait_send())
     chain_drain(weights)
     chain_drain(grads)
 
     def drain(t):
         side_copy(t).wait_send()
         for slot in (1, 0):
-            for k in (0, 1):
+            for k in range(2 + cols):
                 core_copy(t, slot, k).wait_send()
         for lag in range(1, cols):
             for k in range(3):
@@ -1335,6 +1360,8 @@
     _, share, width = grad_rows.shape
     model = w_qkv.shape[1]
     rows = 2 * (grad_up.shape[0] // chain // PARTS)
+    block, done = rows + cols * width // PARTS, rows + width // PARTS
+    local = 3 * width // PARTS
     vmem = pl.BlockSpec(memory_space=pltpu.VMEM)
     anywhere = pl.BlockSpec(memory_space=pl.ANY)
     dma = pltpu.SemaphoreType.DMA
@@ -1344,8 +1371,8 @@
         functools.partial(rear_kernel, n),
         name="rear",
         out_shape=(
-            jax.ShapeDtypeStruct((PARTS, rows, model), BF),
-            jax.ShapeDtypeStruct((PARTS, width, model), BF),
+            jax.ShapeDtypeStruct((PARTS, done, model), BF),
+            jax.ShapeDtypeStruct((PARTS, local, model), BF),
             jax.ShapeDtypeStruct((2, 8, width), F32),
             jax.ShapeDtypeStruct((share, model), BF),
             jax.ShapeDtypeStruct((2, 8, model), F32),
@@ -1360,20 +1387,16 @@
             head,
             head,
             head,
-            pltpu.VMEM((chain, 2, rows, model), BF),
-            pltpu.VMEM((chain * 2 * rows, model), BF),
-            pltpu.VMEM((max(chain * rows, chain * share), model), BF),
-            pltpu.VMEM((2, chain, rows, model), BF),
-            pltpu.VMEM((rows, model), BF),
-            pltpu.VMEM((n, width, model), BF),
-            pltpu.VMEM((PARTS, width, model), BF),
-            pltpu.VMEM((2, width, model), BF),
-            pltpu.VMEM((width, model), BF),
-            pltpu.VMEM((width, model), BF),
+            pltpu.VMEM((chain, 2, block, model), BF),
+            pltpu.VMEM((chain * 2 * block, model), BF),
+            pltpu.VMEM((chain * max(block, share), model), BF),
+            pltpu.VMEM((2, chain, block, model), BF),
+            pltpu.VMEM((cols - 1, width // PARTS, model), BF),
+            pltpu.VMEM((2, local, model), BF),
+            pltpu.VMEM((local, model), BF),
             pltpu.VMEM((3, width, model), F32),
             pltpu.VMEM((cols - 1, 3, chain, share, width), BF),
-            pltpu.VMEM((cols - 1, 3, width, model), BF),
-            pltpu.VMEM((cols - 1, 3, width, model), BF),
+            pltpu.VMEM((cols - 1, 3 * width, model), BF),
             pltpu.VMEM((2, chain, share, model), BF),
             pltpu.VMEM((share, model), F32),
             pltpu.VMEM((2, 3, 8, model), F32),
@@ -1382,11 +1405,11 @@
             pltpu.VMEM((2, 2, 8, width), F32),
             dma((n,)),
             dma((n,)),
-            dma((n,)),
-            dma((n,)),
-            dma((chain, 2, 2)),
-            dma((chain, 2, 2)),
-            dma((chain, 2, 2)),
+            dma((cols,)),
+            dma((cols,)),
+            dma((chain, 2, 2 + cols)),
+            dma((chain, 2, 2 + cols)),
+            dma((chain, 2, 2 + cols)),
             dma((chain,)),
             dma((chain,)),
             dma((2, chain)),
@@ -1532,9 +1555,9 @@
         hidden_sum, head_sum, bias_sum, small = lax.psum((hidden_sum, head_sum, bias_sum, small), "dg")
     half = hidden // PARTS
     grad_w_up = hidden_sum[:, :half].reshape(hidden, model).T.astype(F32)
-    grad_w_down = hidden_sum[:, half:].reshape(hidden, model).astype(F32)
-    grad_w_out = head_sum[0].astype(F32)
-    grad_w_qkv = jnp.transpose(head_sum[1:], (0, 2, 1)).astype(F32)
+    grad_w_down = hidden_sum[:, half : 2 * half].reshape(hidden, model).astype(F32)
+    grad_w_out = hidden_sum[:, 2 * half :].reshape(width, model).astype(F32)
+    grad_w_qkv = jnp.transpose(head_sum.reshape(3, width, model), (0, 2, 1)).astype(F32)
     grad_bias_query, grad_bias_value = bias_sum[:, 0]
     grad_bias_up = lax.dynamic_slice_in_dim(
         small[0, 4:].reshape(-1), model_index * hidden, hidden, 0

time: 359 us -> 343 us (0.955)
  Pallas kernels: 276 us -> 264 us
    pallas_call x1, Pallas kernels: 150 us -> 138 us  [rear(): pl.pallas_call(functools.partial(rear_kernel, n), name='rear', out_shape=...]
  transfers between devices with their start and end apart: 2 -> 2, of which waited for: 1 -> 0; matrix products, arithmetic and copies ran while one was open for 6% -> 7% of each run, Pallas kernels for 0% -> 0%
where the time goes in v1:
time: 343 us; the launch traced here: 340 us
  Pallas kernels  264 us (77%)
  matrix products  41.5 us (12%)
  local copies, waits for them, and re-layouts  19.9 us (6%)
  other arithmetic  11.1 us (3%)
    pallas_call x1, Pallas kernels, rear(): pl.pallas_call(functools.partial(rear_kernel, n), name='rear', out_shape=...  138 us
    pallas_call x1, Pallas kernels, front(): pl.pallas_call(functools.partial(front_kernel, n), name='front', out_shap...  126 us
    dot_general x1, matrix products, body(): jnp.einsum('rd,fd->rf', grad_mlp, down_all, preferred_element_type=F32)  14.5 us
    dot_general x1, matrix products, body(): jnp.einsum('rf,rd->fd', grad_pre, rows_two, preferred_element_type=F32)  7.49 us
  transfers between devices with their start and end apart: 2, of which 0 were waited for; matrix products, arithmetic and copies ran while one was open for 7% of the time, Pallas kernels for 0%

profile of v1, /device:TPU:0, one launch (start us, length us, event | category | flops | bytes accessed | tf_op | source)
XLA Modules:
  0.0 339.5 jit_solution(12053347657891964016)
XLA Ops:
  0.6 0.7 pad_maximum_fusion.2
  1.3 1.3 broadcast_in_dim.11.bup_ref
  3.2 126.3 %front.1 = (bf16[4,288,1024]{2,1,0:T(8,128)(2,1)}, bf16[2,2304,128]{2,1,0:T(8,128)(2,1)}, bf16[2,2304,128]{2,1,0:T(8,128)(2,1)}, bf16[2,2304,128]{2,1,0:T(8,128)...) custom-call(s32[2304]{0:T(1024)} %ids_ref.1, ...), custom_call_target="tpu_custom_call" | custom-call | tf_op jit(solution)/shard_map/front/pallas_call | solution.py:627
  129.6 0.8 slice.47
  130.4 4.9 %fusion.24 = f32[576,2048]{1,0:T(8,128)S(1)} fusion(bf16[576,1024]{1,0:T(8,128)(2,1)} %bitcast.99, bf16[1024,2048]{1,0:T(8,128)(2,1)} %get-tuple-element.35), kind=kOutput, calls=%fused_computation.67 | convolution fusion | flops 2415919104 | bytes 10092544 | tf_op jit(solution)/shard_map/dot_general | solution.py:1506
  135.3 14.5 %convert_reduce_fusion = (f32[2048]{0:T(1024)}, bf16[576,2048]{1,0:T(8,128)(2,1)S(1)}, f32[576,2048]{1,0:T(8,128)S(1)}) fusion(f32[576,2048]{1,0:T(8,128)S(1)} %fusion.24, f32[2048]{0:T(1024)S(1)} %bitcast.88, bf16[576,1024]{1,0:T(8,128)(2,1)S(1)} %bitcast.81, bf16[2048,1024]{1,0:T(8,128)(2,1)S(1)} %copy-done.18), kind=kOutput, calls=%fused_computation.2 | convolution fusion | flops 2504390656 | bytes 17186816 | tf_op jit(solution)/shard_map/rd,fd->rf/dot_general | solution.py:1508
  149.8 2.6 fusion.26
  152.5 0.9 split.40
  153.4 1.4 collective-permute-start.1
  154.8 1.2 multiply_convert_fusion
  156.1 2.6 fusion.25
  158.7 1.0 split.41
  161.5 5.1 %convolution_convert_fusion.refs_15_ = bf16[2048,1024]{1,0:T(8,128)(2,1)} fusion(bf16[576,2048]{1,0:T(8,128)(2,1)S(1)} %multiply_convert_fusion, bf16[576,1024]{1,0:T(8,128)(2,1)S(1)} %bitcast.82), kind=kOutput, calls=%fused_computation.18 | convolution fusion | flops 2418016256 | bytes 7733248 | tf_op jit(solution)/shard_map/rf,rd->fd/dot_general | solution.py:1518
  168.8 1.2 dynamic_update_slice.3
  170.0 0.6 copy.32
  170.6 7.5 %convolution_convert_fusion.1.refs_14_ = bf16[2048,1024]{1,0:T(8,128)(2,1)} fusion(bf16[576,2048]{1,0:T(8,128)(2,1)} %copy-done.22, bf16[576,1024]{1,0:T(8,128)(2,1)} %bitcast.100), kind=kOutput, calls=%fused_computation.19 | convolution fusion | flops 2418016256 | bytes 7733248 | tf_op jit(solution)/shard_map/rf,rd->fd/dot_general | solution.py:1517
  178.3 1.7 multiply_reduce_fusion
  180.0 2.7 fusion.21
  183.1 2.6 convolution_convert_fusion.2
  185.7 1.6 fusion.6.refs_0_
  187.3 0.6 concatenate.3.refs_13_
  188.0 137.6 %rear.1 = (bf16[4,288,1024]{2,1,0:T(8,128)(2,1)}, bf16[4,96,1024]{2,1,0:T(8,128)(2,1)}, f32[2,8,128]{2,1,0:T(8,128)}, bf16[288,1024]{1,0:T(8,128)(2,1)}, f32[2,8,1024]{2,1,0:T(8,128)}) custom-call(bf16[8,288,128]{2,1,0:T(8,128)(2,1)} %fusion.6.refs_0_, bf16[2,2304,128]{2,1,0:T(8,128)(2,1)} %get-tuple-element.40.refs_1_, ...), custom_call_target="tpu_custom_call" | custom-call | tf_op jit(solution)/shard_map/rear/pallas_call | solution.py:1370
  325.5 1.7 fusion.22
  327.3 1.0 slice.52
  328.9 1.9 bitcast_convert_fusion
  330.8 1.8 copy.30
  332.6 1.4 copy.29
  334.0 0.9 bitcast_convert_fusion.2
  334.9 1.2 slice_bitcast_fusion.6
  336.1 0.7 dynamic_slice.3
  336.8 0.6 pad_maximum_fusion
  337.4 1.9 copy.42
  (65 shorter events, 5.7 us)
Async XLA Ops:
  130.4 4.9 %copy-start.4 = (bf16[2,288,1024]{2,1,0:T(8,128)(2,1)S(1)}, bf16[2,288,1024]{2,1,0:T(8,128)(2,1)}, u32[]{:S(2)}) copy-start(bf16[2,288,1024]{2,1,0:T(8,128)(2,1)} %get-tuple-element.39) | copy-start | bytes 3538948
  130.4 4.9 %copy-start.18 = (bf16[2048,1024]{1,0:T(8,128)(2,1)S(1)}, bf16[2048,1024]{1,0:T(8,128)(2,1)}, u32[]{:S(2)}) copy-start(bf16[2048,1024]{1,0:T(8,128)(2,1)} %get-tuple-element.37) | copy-start | bytes 12582916
  135.3 14.5 %copy-start.19 = (bf16[1024,2048]{1,0:T(8,128)(2,1)S(1)}, bf16[1024,2048]{1,0:T(8,128)(2,1)}, u32[]{:S(2)}) copy-start(bf16[1024,2048]{1,0:T(8,128)(2,1)} %get-tuple-element.35) | copy-start | bytes 12582916
  149.8 2.7 copy-start.22
  153.4 24.8 %collective-permute-start.1 = (bf16[288,1024]{1,0:T(8,128)(2,1)}, bf16[288,1024]{1,0:T(8,128)(2,1)}, u32[]{:S(2)}, u32[]{:S(2)}) collective-permute-start(bf16[288,1024]{1,0:T(8,128)(2,1)} %split.40), channel_id=1, source_target_pairs={{0,1},{1,0},{2,3},{3,2},{4,5},{5,4},{6,7},{7,6},{8,9},{9,8},{10,11... | collective-permute-start | bytes 1769480 | tf_op jit(solution)/shard_map/ppermute | solution.py:1472
  156.0 4.3 %copy-start.11 = (f32[2,1024]{1,0:T(2,128)S(1)}, f32[2,1024]{1,0:T(2,128)}, u32[]{:S(2)}) copy-start(f32[2,1024]{1,0:T(2,128)} %gain_ref.1) | copy-start | bytes 24580
  156.0 4.9 %copy-start.14 = (f32[2,1024]{1,0:T(2,128)S(1)}, f32[2,1024]{1,0:T(2,128)}, u32[]{:S(2)}) copy-start(f32[2,1024]{1,0:T(2,128)} %out_bias_ref.1) | copy-start | bytes 24580
  158.7 7.9 %copy-start.2 = (f32[576,1024]{1,0:T(8,128)}, f32[576,1024]{1,0:T(8,128)S(1)}, u32[]{:S(2)}) copy-start(f32[576,1024]{1,0:T(8,128)S(1)} %fusion.25) | copy-start | bytes 7077892
  159.7 20.3 %collective-permute-start = (bf16[288,1024]{1,0:T(8,128)(2,1)}, bf16[288,1024]{1,0:T(8,128)(2,1)}, u32[]{:S(2)}, u32[]{:S(2)}) collective-permute-start(bf16[288,1024]{1,0:T(8,128)(2,1)} %split.41), channel_id=1, source_target_pairs={{0,1},{1,0},{2,3},{3,2},{4,5},{5,4},{6,7},{7,6},{8,9},{9,8},{10,11... | collective-permute-start | bytes 1769480 | tf_op jit(solution)/shard_map/ppermute | solution.py:1472
  161.5 5.1 %copy-start = (f32[288,1024]{1,0:T(8,128)S(1)}, f32[288,1024]{1,0:T(8,128)}, u32[]{:S(2)}) copy-start(f32[288,1024]{1,0:T(8,128)} %get-tuple-element.33) | copy-start | bytes 3538948
  166.7 0.6 copy-start.9
  167.6 0.6 copy-start.15
  170.6 7.5 %copy-start.5 = (bf16[2,288,1024]{2,1,0:T(8,128)(2,1)S(1)}, bf16[2,288,1024]{2,1,0:T(8,128)(2,1)}, u32[]{:S(2)}) copy-start(bf16[2,288,1024]{2,1,0:T(8,128)(2,1)} %get-tuple-element.39) | copy-start | bytes 3538948
  170.6 7.7 %copy-start.8 = (f32[1,1024]{1,0:T(1,128)S(1)}, f32[1,1024]{1,0:T(1,128)}, u32[]{:S(2)}) copy-start(f32[1,1024]{1,0:T(1,128)} %get-tuple-element.74) | copy-start | bytes 12292
  170.6 7.7 %copy-start.10 = (f32[288]{0:T(512)S(1)}, f32[288]{0:T(512)}, u32[]{:S(2)}) copy-start(f32[288]{0:T(512)} %copy-done.9) | copy-start | bytes 3460
  170.6 7.7 %copy-start.13 = (f32[288]{0:T(512)S(1)}, f32[288]{0:T(512)}, u32[]{:S(2)}) copy-start(f32[288]{0:T(512)} %fusion.16) | copy-start | bytes 3460
  170.6 9.4 %copy-start.16 = (f32[288]{0:T(512)S(1)}, f32[288]{0:T(512)}, u32[]{:S(2)}) copy-start(f32[288]{0:T(512)} %copy-done.15) | copy-start | bytes 3460
  170.6 9.4 %copy-start.17 = (f32[1,1024]{1,0:T(1,128)S(1)}, f32[1,1024]{1,0:T(1,128)}, u32[]{:S(2)}) copy-start(f32[1,1024]{1,0:T(1,128)} %slice.48) | copy-start | bytes 12292
  178.1 1.9 copy-start.3
  180.0 3.0 copy-start.21
  182.8 2.9 copy-start.20
  183.0 2.7 copy-start.1
  183.0 4.3 %copy-start.7 = (f32[1,4,2,512]{3,1,2,0:T(4,128)S(1)}, f32[1,4,2,512]{3,1,2,0:T(4,128)}, u32[]{:S(2)}) copy-start(f32[1,4,2,512]{3,1,2,0:T(4,128)} %copy.32) | copy-start | bytes 49156
  325.5 2.7 copy-start.12
  328.9 3.7 %copy-start.6 = (bf16[4,96,1024]{2,1,0:T(8,128)(2,1)S(1)}, bf16[4,96,1024]{2,1,0:T(8,128)(2,1)}, u32[]{:S(2)}) copy-start(bf16[4,96,1024]{2,1,0:T(8,128)(2,1)} %get-tuple-element.50) | copy-start | bytes 2359300
